TPU v7x, 128 devices: a whole 4x4x4 slice. The times are simulated.
128 devices in a mesh: tp: 4 (over x), dp: 32 (over z, y, core).
Axes of the slice: x: 4, y: 4, z: 4, core: 2. Of those that a mesh axis runs over, the one named last changes fastest.
Arguments:
- x_saved: bfloat16 [32, 1024, 2048], P('dp', 'tp')
- dy_out: bfloat16 [32, 1024, 2048], P('dp', 'tp')
- ln_params: float32 [4, 2048], replicated
- w_qkv: bfloat16 [2048, 16, 3, 128], P(None, 'tp')
- w_out: bfloat16 [2048, 2048], P('tp')
- w_up: bfloat16 [2048, 8192], P(None, 'tp')
- w_down: bfloat16 [8192, 2048], P('tp')
Outputs:
- output 1: bfloat16 [32, 1024, 2048], P('dp', 'tp')
- output 2: float32 [4, 2048], replicated
- output 3: float32 [2048, 16, 3, 128], P('dp', 'tp')
- output 4: float32 [2048, 2048], P(('tp', 'dp'))
- output 5: float32 [2048, 8192], P('dp', 'tp')
- output 6: float32 [8192, 2048], P(('tp', 'dp'))
All inputs are finite; a program needn't handle non-finite values.
Results may differ from a plain program's by a relative error of at most 0.0110607.
Values are sent between devices in bfloat16 or wider.
A program may use at most 1 GiB of HBM per device.

v0:
```python
import jax
import jax.numpy as jnp
from jax import lax
from jax.sharding import PartitionSpec as P

NORM_EPS = 1e-5
ROPE_BASE = 10000.0


def layer_norm(x_rows, norm_gain, norm_shift):
    row_mean = jnp.mean(x_rows, axis=-1, keepdims=True)
    centered = x_rows - row_mean
    row_var = jnp.mean(centered * centered, axis=-1, keepdims=True)
    return (centered * lax.rsqrt(row_var + NORM_EPS) * norm_gain + norm_shift).astype(jnp.bfloat16)


def rope_tables(positions, head_dim):
    half_dim = head_dim // 2
    inv_freq = ROPE_BASE ** (-2.0 * jnp.arange(half_dim, dtype=jnp.float32) / head_dim)
    angles = positions.astype(jnp.float32)[:, None] * inv_freq[None, :]
    return jnp.cos(angles), jnp.sin(angles)


def apply_rope(tensor, cos_t, sin_t):
    half_dim = tensor.shape[-1] // 2
    t_f32 = tensor.astype(jnp.float32)
    lo_half = t_f32[..., :half_dim]
    hi_half = t_f32[..., half_dim:]
    return jnp.concatenate([lo_half * cos_t - hi_half * sin_t, hi_half * cos_t + lo_half * sin_t], axis=-1).astype(jnp.bfloat16)


def gelu_bf16(hidden):
    return jax.nn.gelu(hidden.astype(jnp.float32), approximate=False).astype(jnp.bfloat16)


def attention_core(qkv_proj, cos_t, sin_t):
    q_slots = qkv_proj.shape[3] - 2
    positions = jnp.arange(qkv_proj.shape[1])
    rotated = apply_rope(qkv_proj[:, :, :, :q_slots + 1, :], cos_t[:, None, None, :], sin_t[:, None, None, :])
    query_rot = rotated[:, :, :, :q_slots, :]
    key_rot = rotated[:, :, :, q_slots, :]
    values = qkv_proj[:, :, :, q_slots + 1, :]
    scores = jnp.einsum('btgqh,bsgh->bgqts', query_rot, key_rot, preferred_element_type=jnp.float32) * (qkv_proj.shape[4] ** -0.5)
    causal = positions[:, None] >= positions[None, :]
    attn_probs = jax.nn.softmax(jnp.where(causal, scores, -1e30), axis=-1).astype(jnp.bfloat16)
    return jnp.einsum('bgqts,bsgh->btgqh', attn_probs, values, preferred_element_type=jnp.float32).astype(jnp.bfloat16)


def solution(mesh):
    def local_step(x_loc, dy_loc, ln_params, w_qkv, w_out, w_up, w_down):
        x_full = lax.all_gather(x_loc, 'tp', axis=1, tiled=True)
        x_full_f32 = x_full.astype(jnp.float32)
        h_attn = layer_norm(x_full_f32, ln_params[0], ln_params[1])
        h_mlp = layer_norm(x_full_f32, ln_params[2], ln_params[3])
        qkv_proj = jnp.einsum('btd,dgjh->btgjh', h_attn, w_qkv, preferred_element_type=jnp.float32).astype(jnp.bfloat16)
        cos_t, sin_t = rope_tables(jnp.arange(x_full.shape[1]), w_qkv.shape[3])
        context, attn_pull = jax.vjp(lambda qkv_in: attention_core(qkv_in, cos_t, sin_t), qkv_proj)
        hidden = jnp.einsum('btd,df->btf', h_mlp, w_up, preferred_element_type=jnp.float32).astype(jnp.bfloat16)
        gelu_out, gelu_pull = jax.vjp(gelu_bf16, hidden)
        dy_full = lax.all_gather(dy_loc, 'tp', axis=1, tiled=True)
        num_seqs, seq_len = dy_full.shape[0], dy_full.shape[1]
        d_ctx = jnp.einsum('btd,cd->btc', dy_full, w_out, preferred_element_type=jnp.float32).astype(jnp.bfloat16)
        g_wout = jnp.einsum('btc,btd->cd', context.reshape(num_seqs, seq_len, -1), dy_full, preferred_element_type=jnp.float32)
        (d_proj,) = attn_pull(d_ctx.reshape(context.shape))
        g_wqkv = jnp.einsum('btd,btgjh->dgjh', h_attn, d_proj, preferred_element_type=jnp.float32)
        d_hattn_part = jnp.einsum('btgjh,dgjh->btd', d_proj, w_qkv, preferred_element_type=jnp.float32).astype(jnp.bfloat16)
        d_gelu = jnp.einsum('btd,fd->btf', dy_full, w_down, preferred_element_type=jnp.float32).astype(jnp.bfloat16)
        g_wdown = jnp.einsum('btf,btd->fd', gelu_out, dy_full, preferred_element_type=jnp.float32)
        (d_hidden,) = gelu_pull(d_gelu)
        g_wup = jnp.einsum('btd,btf->df', h_mlp, d_hidden, preferred_element_type=jnp.float32)
        d_hmlp_part = jnp.einsum('btf,df->btd', d_hidden, w_up, preferred_element_type=jnp.float32).astype(jnp.bfloat16)
        d_hattn = lax.psum_scatter(d_hattn_part, 'tp', scatter_dimension=1, tiled=True)
        d_hmlp = lax.psum_scatter(d_hmlp_part, 'tp', scatter_dimension=1, tiled=True)
        x_loc_f32 = x_loc.astype(jnp.float32)
        _, attn_norm_pull = jax.vjp(layer_norm, x_loc_f32, ln_params[0], ln_params[1])
        _, mlp_norm_pull = jax.vjp(layer_norm, x_loc_f32, ln_params[2], ln_params[3])
        dx_attn, dgain_attn, dshift_attn = attn_norm_pull(d_hattn)
        dx_mlp, dgain_mlp, dshift_mlp = mlp_norm_pull(d_hmlp)
        grad_x = (dy_loc.astype(jnp.float32) + dx_attn + dx_mlp).astype(jnp.bfloat16)
        grad_ln = lax.psum(jnp.stack([dgain_attn, dshift_attn, dgain_mlp, dshift_mlp]), ('tp', 'dp'))
        grad_wqkv = lax.psum_scatter(g_wqkv, 'dp', scatter_dimension=0, tiled=True)
        grad_wout = lax.psum_scatter(g_wout, 'dp', scatter_dimension=0, tiled=True)
        grad_wup = lax.psum_scatter(g_wup, 'dp', scatter_dimension=0, tiled=True)
        grad_wdown = lax.psum_scatter(g_wdown, 'dp', scatter_dimension=0, tiled=True)
        return grad_x, grad_ln, grad_wqkv, grad_wout, grad_wup, grad_wdown

    act_spec = P('dp', 'tp', None)
    in_specs = (act_spec, act_spec, P(None, None), P(None, 'tp', None, None), P('tp', None), P(None, 'tp'), P('tp', None))
    out_specs = (act_spec, P(None, None), P('dp', 'tp', None, None), P(('tp', 'dp'), None), P('dp', 'tp'), P(('tp', 'dp'), None))
    return jax.shard_map(local_step, mesh=mesh, in_specs=in_specs, out_specs=out_specs, check_vma=False)
```

profile of v0, /device:TPU:0, one launch (start us, length us, event | category | flops | bytes accessed | tf_op | source)
XLA Modules:
  0.0 722.6 jit_solution(12382001578886554522)
XLA Ops:
  10.6 10.7 %copy.13 = bf16[2048,4,3,128]{0,3,2,1:T(8,128)(2,1)} copy(bf16[2048,4,3,128]{3,1,2,0:T(4,128)(2,1)} %param.10) | data formatting | bytes 12582912 | tf_op args[3]
  23.0 37.2 %all-gather.5.cloned.1.call-done = bf16[1,1024,2048]{2,1,0:T(8,128)(2,1)} async-done(((bf16[1,256,2048]{2,1,0:T(8,128)(2,1)}), bf16[1,1024,2048]{2,1,0:T(8,128)(2,1)}) %all-gather.5.cloned.1.call-update) | async-done | bytes 4194320 | tf_op jit(solution)/shard_map/all_gather | solution.py:51
  60.2 3.0 convert_reduce_fusion
  63.2 3.4 fusion.20
  66.6 9.4 %fusion.70 = f32[1024,1536]{0,1:S(1)} fusion(bf16[2048,1536]{0,1:T(8,128)(2,1)} %bitcast.185, bf16[1,1024,2048]{2,1,0:T(8,128)(2,1)S(1)} %copy-done.4, f32[2048]{0:T(1024)S(1)} %bitcast.205, f32[2048]{0:T(1024)S(1)} %bitcast.194, f32[1024]{0:T(1024)S(1)} %add_rsqrt_fusion, f32[1024]{0:T(1024)S(1)} %broadcast_multiply_fusion), kind=kOutput, calls=%fused_computation.81 | convolution fusion | flops 6455033856 | bytes 16801792
  78.4 3.3 fusion.9
  81.7 3.8 fusion.140
  85.6 1.8 copy-done.3
  87.5 22.9 %all-gather.3.cloned.1.call-done = bf16[1,1024,2048]{2,1,0:T(8,128)(2,1)} async-done(((bf16[1,256,2048]{2,1,0:T(8,128)(2,1)}), bf16[1,1024,2048]{2,1,0:T(8,128)(2,1)}) %all-gather.3.cloned.1.call-update) | async-done | bytes 4194320 | tf_op jit(solution)/shard_map/all_gather | solution.py:60
  110.3 4.5 fusion.104
  114.9 10.0 %fusion.119 = bf16[1,1024,4,1,128]{1,4,3,2,0:T(8,128)(2,1)} fusion(bf16[4,128,1024]{2,1,0:T(8,128)(2,1)S(1)} %bitcast.208, f32[4,1024]{1,0:T(4,128)S(1)} %fusion.140, f32[4,1024]{1,0:T(4,128)S(1)} %get-tuple-element.36, f32[4,1024,1024]{2,1,0:T(8,128)} %copy-done.3, pred[1024,1024]{0,1:T(8,128)(4,1)S(1)} %iota_compare_fusion), kind=kOutput, calls=%fused_computation.139 | convolution fusion | flops 1095237632 | bytes 19955712 | tf_op jit(solution)/shard_map/transpose(jvp(bgqts,bsgh->btgqh))/dot_general | solution.py:46
  124.8 10.2 %fusion.8 = (f32[4,1024]{1,0:T(4,128)S(1)}, bf16[4,1024,1024]{1,2,0:T(8,128)(2,1)S(1)}) fusion(f32[4,1024]{1,0:T(4,128)S(1)} %multiply_divide_fusion, f32[4,1024]{1,0:T(4,128)S(1)} %get-tuple-element.36, f32[4,1024,1024]{2,1,0:T(8,128)} %copy-done.3, pred[1024,1024]{0,1:T(8,128)(4,1)S(1)} %iota_compare_fusion, bf16[4,128,1024]{2,1,0:T(8,128)(2,1)S(1)} %bitcast.209, ...), kind=kOutput, calls=%fused_computation.10 | convolution fusion | flops 1107292160 | bytes 28360704 | tf_op jit(solution)/shard_map/transpose(jvp(bgqts,bsgh->btgqh))/dot_general | solution.py:46
  135.1 10.9 %fusion.116 = bf16[1,1024,4,1,128]{1,4,3,2,0:T(8,128)(2,1)S(1)} fusion(bf16[4,1024,1024]{1,2,0:T(8,128)(2,1)S(1)} %get-tuple-element.39, f32[4,1024]{1,0:T(4,128)S(1)} %neg.28, f32[4,1024]{1,0:T(4,128)S(1)} %fusion.140, pred[1024,1024]{0,1:T(8,128)(4,1)S(1)} %iota_compare_fusion, bf16[1,1024,4,2,64]{1,4,3,2,0:T(8,128)(2,1)S(1)} %copy-done.13, ...), kind=kOutput, calls=%fused_computation.138 | convolution fusion | flops 1114112000 | bytes 29409280 | tf_op jit(solution)/shard_map/transpose(jvp(btgqh,bsgh->bgqts))/dot_general | solution.py:43
  146.0 11.8 %fusion.113 = bf16[1,1024,4,1,128]{1,4,3,2,0:T(8,128)(2,1)S(1)} fusion(bf16[4,1024,1024]{1,2,0:T(8,128)(2,1)S(1)} %get-tuple-element.39, f32[4,1024]{1,0:T(4,128)S(1)} %neg.28, f32[4,1024]{1,0:T(4,128)S(1)} %fusion.140, pred[1024,1024]{0,1:T(8,128)(4,1)S(1)} %iota_compare_fusion, f32[4,1024,1024]{2,1,0:T(8,128)} %copy-done.3, ...), kind=kOutput, calls=%fused_computation.137 | convolution fusion | flops 1114112000 | bytes 29409280 | tf_op jit(solution)/shard_map/transpose(jvp(btgqh,bsgh->bgqts))/dot_general | solution.py:43
  161.8 8.4 %fusion.82 = bf16[1,1024,2048]{2,1,0:T(8,128)(2,1)} fusion(bf16[2048,4,3,128]{0,3,2,1:T(8,128)(2,1)S(1)} %bitcast.187, bf16[1,1024,4,2,128]{1,4,3,2,0:T(8,128)(2,1)S(1)} %add_convert_fusion, bf16[1,1024,4,1,128]{1,4,3,2,0:T(8,128)(2,1)S(1)} %copy-done.23), kind=kOutput, calls=%fused_computation.95 | convolution fusion | flops 6446120960 | bytes 13631488 | tf_op jit(solution)/shard_map/btgjh,dgjh->btd/dot_general | solution.py:66
  170.3 32.6 %fusion.49 = (f32[1024,2048]{1,0:T(8,128)}, bf16[1024,2048]{1,0:T(8,128)(2,1)S(1)}) fusion(bf16[2048,2048]{1,0:T(8,128)(2,1)} %param.12, bf16[1,1024,2048]{2,1,0:T(8,128)(2,1)} %all-gather.5.cloned.1.call-done, f32[2048]{0:T(1024)S(1)} %bitcast.203, f32[2048]{0:T(1024)S(1)} %bitcast.189, f32[1024]{0:T(1024)S(1)} %add_rsqrt_fusion, ...), kind=kOutput, calls=%fused_computation.61 | convolution fusion | flops 8736735232 | bytes 25190400 | tf_op jit(solution)/shard_map/btd,df->btf/dot_general | solution.py:58
  202.9 18.5 %fusion.55 = bf16[1024,2048]{1,0:T(8,128)(2,1)} fusion(bf16[1024,2048]{1,0:T(8,128)(2,1)S(1)} %get-tuple-element.41, f32[1024,2048]{1,0:T(8,128)} %get-tuple-element.40, bf16[2048,2048]{1,0:T(8,128)(2,1)} %param.13, bf16[1,1024,2048]{2,1,0:T(8,128)(2,1)S(1)} %copy-done.20), kind=kOutput, calls=%fused_computation.67 | convolution fusion | flops 8625586176 | bytes 29360128 | tf_op jit(solution)/shard_map/btd,fd->btf/dot_general | solution.py:67
  221.4 14.0 %convert_bitcast_fusion = bf16[1,1024,2048]{2,1,0:T(8,128)(2,1)} fusion(bf16[1024,2048]{1,0:T(8,128)(2,1)} %fusion.55, bf16[2048,2048]{1,0:T(8,128)(2,1)} %param.12), kind=kOutput, calls=%fused_computation.90 | convolution fusion | flops 8592031744 | bytes 16777216 | tf_op jit(solution)/shard_map/btf,df->btd/dot_general | solution.py:71
  235.5 12.1 %fusion.68 = f32[2048,4,3,128]{3,0,2,1:T(8,128)} fusion(bf16[1,1024,4,2,128]{1,4,3,2,0:T(8,128)(2,1)S(1)} %copy-done.9, bf16[1,1024,4,1,128]{1,4,3,2,0:T(8,128)(2,1)} %fusion.119, bf16[1,1024,2048]{2,1,0:T(8,128)(2,1)} %all-gather.5.cloned.1.call-done, f32[2048]{0:T(1024)S(1)} %bitcast.206, f32[2048]{0:T(1024)S(1)} %bitcast.195, ...), kind=kOutput, calls=%fused_computation.79 | convolution fusion | flops 6461325312 | bytes 19947520 | tf_op jit(solution)/shard_map/btd,btgjh->dgjh/dot_general | solution.py:65
  247.7 9.4 %fusion.110 = bf16[4,128,1024]{2,1,0:T(8,128)(2,1)S(1)} fusion(bf16[1,1024,4,3,128]{1,4,3,2,0:T(8,128)(2,1)} %copy-done.5, f32[4,1024]{1,0:T(4,128)S(1)} %fusion.140, f32[4,1024]{1,0:T(4,128)S(1)} %get-tuple-element.36, f32[4,1024,1024]{2,1,0:T(8,128)} %copy-done.3, pred[1024,1024]{0,1:T(8,128)(4,1)S(1)} %iota_compare_fusion), kind=kOutput, calls=%fused_computation.136 | convolution fusion | flops 1095237632 | bytes 19955712 | tf_op jit(solution)/shard_map/jvp(bgqts,bsgh->btgqh)/dot_general | solution.py:46
  257.1 4.3 fusion.73
  261.4 15.7 %fusion.143 = f32[2048,2048]{1,0:T(8,128)} fusion(bf16[1024,2048]{1,0:T(8,128)(2,1)} %fusion.55, bf16[1,1024,2048]{2,1,0:T(8,128)(2,1)} %all-gather.5.cloned.1.call-done, f32[2048]{0:T(1024)S(1)} %bitcast.204, f32[2048]{0:T(1024)S(1)} %bitcast.190, f32[1024]{0:T(1024)S(1)} %add_rsqrt_fusion, f32[1024]{0:T(1024)S(1)} %broadcast_multiply_fusion), kind=kOutput, calls=%fused_computation.174 | convolution fusion | flops 8602517504 | bytes 25190400 | tf_op jit(solution)/shard_map/btd,btf->df/dot_general | solution.py:70
  277.2 16.8 %fusion.65 = f32[2048,2048]{1,0:T(8,128)} fusion(f32[1024,2048]{1,0:T(8,128)} %get-tuple-element.40, bf16[1024,2048]{1,0:T(8,128)(2,1)} %copy-done.22, bf16[1,1024,2048]{2,1,0:T(8,128)(2,1)} %all-gather.3.cloned.1.call-done), kind=kOutput, calls=%fused_computation.77 | convolution fusion | flops 8598323200 | bytes 33554432 | tf_op jit(solution)/shard_map/btf,btd->fd/dot_general | solution.py:68
  295.5 2.9 fusion.94
  298.4 3.4 fusion.96
  301.9 66.2 %psum.7 = f32[4,2048]{1,0:T(4,128)} all-reduce(f32[4,2048]{1,0:T(4,128)S(1)} %pad_maximum_fusion.1), channel_id=1, replica_groups=mesh['tp'=4,'dp'=32] {'tp','dp'}, use_global_device_ids=true, to_apply=%region_17.18 | all-reduce | flops 8192 | bytes 65536 | tf_op jit(solution)/shard_map/psum | solution.py:80
  368.1 4.3 add_convert_fusion.1
  372.3 19.0 %reduce-scatter.11.cloned.1.call-done = f32[64,4,3,128]{3,0,2,1:T(8,128)} async-done(((f32[2048,4,3,128]{3,0,2,1:T(8,128)}), f32[64,4,3,128]{3,0,2,1:T(8,128)}) %reduce-scatter.11.cloned.1.call-update) | async-done | bytes 393232 | tf_op jit(solution)/shard_map/reduce_scatter | solution.py:81
  391.4 2.0 copy.23
  393.4 83.7 %reduce-scatter.13.cloned.1.call-done = f32[16,2048]{1,0:T(8,128)} async-done(((f32[512,2048]{1,0:T(8,128)}), f32[16,2048]{1,0:T(8,128)}) %reduce-scatter.13.cloned.1.call-update) | async-done | bytes 131088 | tf_op jit(solution)/shard_map/reduce_scatter | solution.py:82
  477.1 119.1 %reduce-scatter.15.cloned.1.call-done = f32[64,2048]{1,0:T(8,128)} async-done(((f32[2048,2048]{1,0:T(8,128)}), f32[64,2048]{1,0:T(8,128)}) %reduce-scatter.15.cloned.1.call-update) | async-done | bytes 524304 | tf_op jit(solution)/shard_map/reduce_scatter | solution.py:83
  596.2 119.1 %reduce-scatter.17.cloned.1.call-done = f32[64,2048]{1,0:T(8,128)} async-done(((f32[2048,2048]{1,0:T(8,128)}), f32[64,2048]{1,0:T(8,128)}) %reduce-scatter.17.cloned.1.call-update) | async-done | bytes 524304 | tf_op jit(solution)/shard_map/reduce_scatter | solution.py:84
  (91 shorter events, 13.2 us)
Async XLA Ops:
  7.2 103.2 %copy-start = (bf16[512,2048]{1,0:T(8,128)(2,1)S(1)}, bf16[512,2048]{1,0:T(8,128)(2,1)}, u32[]{:S(2)}) copy-start(bf16[512,2048]{1,0:T(8,128)(2,1)} %param.11) | copy-start | bytes 6291460
  7.2 53.0 %all-gather.5.cloned.1.call-start = ((), (), s32[]{:S(2)}) async-start(), calls=%async_computation.7 | async-start | bytes 5242880 | tf_op jit(solution)/shard_map/all_gather | solution.py:51
  7.9 102.4 %all-gather.3.cloned.1.call-start = ((), (), s32[]{:S(2)}) async-start(), calls=%async_computation.6 | async-start | bytes 5242880 | tf_op jit(solution)/shard_map/all_gather | solution.py:60
  8.7 286.8 %reduce-scatter.7.cloned.1.call-start = ((), (), s32[]{:S(2)}) async-start(), calls=%async_computation.8 | async-start | bytes 5242880 | tf_op jit(solution)/shard_map/reduce_scatter | solution.py:72
  10.6 56.0 %copy-start.15 = (f32[1,2048]{1,0:T(1,128)}, f32[1,2048]{1,0:T(1,128)S(1)}, u32[]{:S(2)}) copy-start(f32[1,2048]{1,0:T(1,128)S(1)} %get-tuple-element.31) | copy-start | bytes 24580
  10.6 56.0 %copy-start.18 = (f32[1,2048]{1,0:T(1,128)}, f32[1,2048]{1,0:T(1,128)S(1)}, u32[]{:S(2)}) copy-start(f32[1,2048]{1,0:T(1,128)S(1)} %get-tuple-element.30) | copy-start | bytes 24580
  60.2 6.4 copy-start.4
  76.6 1.8 copy-start.5
  77.8 4.0 copy-start.10
  77.8 3.9 copy-start.12
  81.7 5.7 copy-start.3
  124.8 10.2 %copy-start.11 = (bf16[1,1024,4,2,64]{1,4,3,2,0:T(8,128)(2,1)S(1)}, bf16[1,1024,4,2,64]{1,4,3,2,0:T(8,128)(2,1)}, u32[]{:S(2)}) copy-start(bf16[1,1024,4,2,64]{1,4,3,2,0:T(8,128)(2,1)} %copy-done.10) | copy-start | bytes 3145732
  124.8 10.2 %copy-start.13 = (bf16[1,1024,4,2,64]{1,4,3,2,0:T(8,128)(2,1)S(1)}, bf16[1,1024,4,2,64]{1,4,3,2,0:T(8,128)(2,1)}, u32[]{:S(2)}) copy-start(bf16[1,1024,4,2,64]{1,4,3,2,0:T(8,128)(2,1)} %copy-done.12) | copy-start | bytes 3145732
  146.0 12.1 %copy-start.7 = (f32[1024,64]{0,1:T(8,128)S(1)}, f32[1024,64]{0,1:T(8,128)}, u32[]{:S(2)}) copy-start(f32[1024,64]{0,1:T(8,128)} %get-tuple-element.34) | copy-start | bytes 786436
  157.9 2.9 slice-start
  158.2 3.1 slice-start.1
  158.2 3.6 copy-start.23
  159.5 1.3 copy-start.8
  161.8 8.4 %copy-start.14 = (f32[1,2048]{1,0:T(1,128)S(1)}, f32[1,2048]{1,0:T(1,128)}, u32[]{:S(2)}) copy-start(f32[1,2048]{1,0:T(1,128)} %get-tuple-element.29) | copy-start | bytes 24580
  161.8 8.5 %copy-start.17 = (f32[1,2048]{1,0:T(1,128)S(1)}, f32[1,2048]{1,0:T(1,128)}, u32[]{:S(2)}) copy-start(f32[1,2048]{1,0:T(1,128)} %get-tuple-element.32) | copy-start | bytes 24580
  170.2 125.3 %reduce-scatter.9.cloned.1.call-start = ((), (), s32[]{:S(2)}) async-start(), calls=%async_computation.9 | async-start | bytes 5242880 | tf_op jit(solution)/shard_map/reduce_scatter | solution.py:73
  170.2 32.7 %copy-start.20 = (bf16[1,1024,2048]{2,1,0:T(8,128)(2,1)S(1)}, bf16[1,1024,2048]{2,1,0:T(8,128)(2,1)}, u32[]{:S(2)}) copy-start(bf16[1,1024,2048]{2,1,0:T(8,128)(2,1)} %all-gather.3.cloned.1.call-done) | copy-start | bytes 12582916
  202.9 18.5 %copy-start.22 = (bf16[1024,2048]{1,0:T(8,128)(2,1)}, bf16[1024,2048]{1,0:T(8,128)(2,1)S(1)}, u32[]{:S(2)}) copy-start(bf16[1024,2048]{1,0:T(8,128)(2,1)S(1)} %get-tuple-element.41) | copy-start | bytes 12582916
  221.4 14.1 %copy-start.9 = (bf16[1,1024,4,2,128]{1,4,3,2,0:T(8,128)(2,1)S(1)}, bf16[1,1024,4,2,128]{1,4,3,2,0:T(8,128)(2,1)}, u32[]{:S(2)}) copy-start(bf16[1,1024,4,2,128]{1,4,3,2,0:T(8,128)(2,1)} %copy-done.8) | copy-start | bytes 6291460
  221.4 14.1 %copy-start.16 = (f32[1,2048]{1,0:T(1,128)S(1)}, f32[1,2048]{1,0:T(1,128)}, u32[]{:S(2)}) copy-start(f32[1,2048]{1,0:T(1,128)} %copy-done.15) | copy-start | bytes 24580
  221.4 14.1 %copy-start.19 = (f32[1,2048]{1,0:T(1,128)S(1)}, f32[1,2048]{1,0:T(1,128)}, u32[]{:S(2)}) copy-start(f32[1,2048]{1,0:T(1,128)} %copy-done.18) | copy-start | bytes 24580
  235.5 155.9 %reduce-scatter.11.cloned.1.call-start = ((), (), s32[]{:S(2)}) async-start(), calls=%async_computation.10 | async-start | bytes 12976128 | tf_op jit(solution)/shard_map/reduce_scatter | solution.py:81
  247.6 229.5 %reduce-scatter.13.cloned.1.call-start = ((), (), s32[]{:S(2)}) async-start(), calls=%async_computation.11 | async-start | bytes 4325376 | tf_op jit(solution)/shard_map/reduce_scatter | solution.py:82
  247.7 9.4 %copy-start.21 = (bf16[1,1024,2048]{2,1,0:T(8,128)(2,1)S(1)}, bf16[1,1024,2048]{2,1,0:T(8,128)(2,1)}, u32[]{:S(2)}) copy-start(bf16[1,1024,2048]{2,1,0:T(8,128)(2,1)} %all-gather.3.cloned.1.call-done) | copy-start | bytes 12582916
  261.3 334.8 %reduce-scatter.15.cloned.1.call-start = ((), (), s32[]{:S(2)}) async-start(), calls=%async_computation.12 | async-start | bytes 17301504 | tf_op jit(solution)/shard_map/reduce_scatter | solution.py:83
  277.1 438.2 %reduce-scatter.17.cloned.1.call-start = ((), (), s32[]{:S(2)}) async-start(), calls=%async_computation.13 | async-start | bytes 17301504 | tf_op jit(solution)/shard_map/reduce_scatter | solution.py:84
  295.2 420.1 %copy-start.1 = (bf16[512,2048]{1,0:T(8,128)(2,1)S(1)}, bf16[512,2048]{1,0:T(8,128)(2,1)}, u32[]{:S(2)}) copy-start(bf16[512,2048]{1,0:T(8,128)(2,1)} %param.11) | copy-start | bytes 6291460
  (2 other events, 2.2 us)
Sparse Core Ops, SparseCore 0:
  9.7 50.5 all-gather.4
  61.9 48.4 all-gather.2
  170.3 47.2 reduce-scatter.6
  235.6 47.2 reduce-scatter.8
  286.6 104.7 reduce-scatter.10
  395.4 81.6 reduce-scatter.12
  481.6 114.5 reduce-scatter.14
  600.6 114.5 reduce-scatter.16
where the time goes:
time: 732 us; the launch traced here: 723 us
  waiting for transfers between devices  403 us (55%)
  matrix products  192 us (26%)
  blocking collectives  66.2 us (9%)
  other arithmetic  26.4 us (4%)
  local copies, waits for them, and re-layouts  20.2 us (3%)
  between operations  15 us (2%)
    reduce_scatter x1, waiting for transfers between devices, local_step(): lax.psum_scatter(g_wdown, 'dp', scatter_dimension=0, tiled=True)  119 us
    reduce_scatter x1, waiting for transfers between devices, local_step(): grad_wup = lax.psum_scatter(g_wup, 'dp', scatter_dimension=0, tiled=True)  119 us
    reduce_scatter x1, waiting for transfers between devices, local_step(): grad_wout = lax.psum_scatter(g_wout, 'dp', scatter_dimension=0, tiled=True)  83.7 us
    psum x1, blocking collectives, local_step(): lax.psum(jnp.stack([dgain_attn, dshift_attn, dgain_mlp, dshift_mlp]), ('t...  66.2 us
    all_gather x1, waiting for transfers between devices, local_step(): x_full = lax.all_gather(x_loc, 'tp', axis=1, tiled=True)  37.2 us
    dot_general x1, matrix products, local_step(): jnp.einsum('btd,df->btf', h_mlp, w_up, preferred_element_type=jnp.float32)  32.6 us
    dot_general x3, matrix products, attention_core(): jnp.einsum('bgqts,bsgh->btgqh', attn_probs, values, preferred_element_typ...  29.5 us
    dot_general x3, matrix products, attention_core(): jnp.einsum('btgqh,bsgh->bgqts', query_rot, key_rot, preferred_element_typ...  26.1 us
  transfers between devices with their start and end apart: 8, of which 6 were waited for; matrix products, arithmetic and copies ran while one was open for 24% of the time, Pallas kernels for 0%

commit v1 on v0

v1 whole, which is shorter than its diff:
```python
import functools

import jax
import jax.numpy as jnp
import numpy as np
from jax import lax
from jax.experimental import pallas as pl
from jax.experimental.pallas import tpu as pltpu
from jax.sharding import PartitionSpec as P

NORM_EPS = 1e-5
ROPE_BASE = 10000.0
MESH = pl.DeviceIdType.MESH
PIECES = 24
SLOTS = 8
STEPS = PIECES + 7
F32 = jnp.float32
BF16 = jnp.bfloat16


def rope_tables(seq_len, head_dim):
    half_dim = head_dim // 2
    inv_freq = np.float32(ROPE_BASE) ** (np.float32(-2.0) * np.arange(half_dim, dtype=np.float32) / np.float32(head_dim))
    angles = np.arange(seq_len, dtype=np.float32)[:, None] * inv_freq[None, :].astype(np.float32)
    cos_t, sin_t = np.cos(angles), np.sin(angles)
    return np.concatenate([cos_t, cos_t], axis=1), np.concatenate([-sin_t, sin_t], axis=1)


def dot_nn(lhs, rhs):
    return lax.dot_general(lhs, rhs, (((1,), (0,)), ((), ())), preferred_element_type=F32)


def dot_nt(lhs, rhs):
    return lax.dot_general(lhs, rhs, (((1,), (1,)), ((), ())), preferred_element_type=F32)


def dot_tt(lhs, rhs):
    return lax.dot_general(lhs, rhs, (((0,), (0,)), ((), ())), preferred_element_type=F32)


def front_kernel(x_ref, dy_ref, ln_ref, cos_ref, sin_ref, wq_ref, wu_ref, wd_ref, wo_ref,
                 o_x, o_dy, o_ha, o_hm, o_qkv, o_gelu, o_dhid, o_dctx, o_w, mean_ref, rstd_ref,
                 x_v, dy_v, w2, wu, wd, wo, wq_b, wq_f, slope, ha, hm, hat, hmt, get, qkv, dh, dc,
                 xs, xr, ds, dr, in_sem, wq_sem, out_sem, fin_sem):
    tp = lax.axis_index('tp')
    nxt, opp, prv = lax.rem(tp + 1, 4), lax.rem(tp + 2, 4), lax.rem(tp + 3, 4)
    d_model = x_ref.shape[1]
    rows = x_ref.shape[0]
    half = rows // 2
    part = wq_b.shape[1]
    barrier = pltpu.get_barrier_semaphore()
    for peer in (nxt, prv):
        pl.semaphore_signal(barrier, inc=1, device_id={'tp': peer}, device_id_type=MESH)

    def wq_copy(i):
        return pltpu.make_async_copy(wq_ref.at[pl.ds(i * part, part)], wq_b.at[i % 2], wq_sem.at[i % 2])

    loads = [pltpu.make_async_copy(x_ref, x_v.at[tp], in_sem.at[0]), pltpu.make_async_copy(dy_ref, dy_v.at[tp], in_sem.at[1]),
             pltpu.make_async_copy(wu_ref, wu, in_sem.at[2]), pltpu.make_async_copy(wd_ref, wd, in_sem.at[3]),
             pltpu.make_async_copy(wo_ref, wo, in_sem.at[4])]
    wq_copy(0).start()
    loads[0].start()
    wq_copy(1).start()
    loads[2].start()
    loads[1].start()
    loads[3].start()
    loads[4].start()
    pl.semaphore_wait(barrier, 2)

    A, B = pl.ds(0, half), pl.ds(half, half)

    def moves(src, buf, ssem, rsem):
        def one(i, ref, slot, piece, to):
            return pltpu.make_async_remote_copy(src_ref=ref, dst_ref=buf.at[slot, piece], send_sem=ssem.at[i], recv_sem=rsem.at[i],
                                                device_id={'tp': to}, device_id_type=MESH)
        return [one(0, src.at[A], tp, A, nxt), one(1, src.at[B], tp, B, prv), one(2, src.at[B], tp, B, nxt), one(3, src.at[A], tp, A, prv),
                one(4, buf.at[prv, A], prv, A, nxt), one(5, buf.at[nxt, B], nxt, B, prv)]

    xm = moves(x_ref, x_v, xs, xr)
    dm = moves(dy_ref, dy_v, ds, dr)
    for i in range(4):
        xm[i].start()

    per = part // 12
    for i in range(wq_ref.shape[0] // part):
        wq_copy(i).wait()

        @pl.loop(0, part // 256)
        def _(r):
            at = pl.ds(pl.multiple_of(r * 256, 256), 256)
            wq_f[at, :] = wq_b[i % 2, at, :].astype(F32)

        if i + 2 < wq_ref.shape[0] // part:
            wq_copy(i + 2).start()
        for j in range(3):
            for g in range(4):
                w2[i * per:(i + 1) * per, g * 384 + j * 128:g * 384 + j * 128 + 128] = wq_f[pl.ds(j * 4 + g, per, stride=12), :].astype(BF16)
    w_out_copy = pltpu.make_async_copy(w2, o_w, fin_sem.at[8])
    w_out_copy.start()

    outs = {}

    def start(kind, n, src, dst):
        copy = pltpu.make_async_copy(src, dst, out_sem.at[kind, n % 2])
        copy.start()
        outs[kind, n % 2] = copy

    def put(kind, n, buf, ref, slot):
        start(kind, n, buf.at[n % 2], ref.at[pl.ds(pl.multiple_of(slot * rows, rows), rows)])

    def put_t(kind, buf, ref, slot):
        start(kind, 0, buf, ref.at[:, pl.ds(pl.multiple_of(slot * rows, rows), rows)])

    def free(kind, n):
        if (kind, n % 2) in outs:
            outs.pop((kind, n % 2)).wait()

    def forward(slot, n):
        s = n % 2
        base = slot * rows

        @pl.loop(0, rows // 32)
        def _(r):
            at = pl.ds(pl.multiple_of(r * 32, 32), 32)
            to = pl.ds(pl.multiple_of(base + r * 32, 32), 32)
            xf = x_v[slot, at, :].astype(F32)
            mean = jnp.mean(xf, axis=-1, keepdims=True)
            cen = xf - mean
            rstd = lax.rsqrt(jnp.mean(cen * cen, axis=-1, keepdims=True) + NORM_EPS)
            mean_ref[to, :] = mean
            rstd_ref[to, :] = rstd
            x_hat = cen * rstd
            ha[at, :] = (x_hat * ln_ref[0:1, :] + ln_ref[1:2, :]).astype(BF16)
            hm[at, :] = (x_hat * ln_ref[2:3, :] + ln_ref[3:4, :]).astype(BF16)

        for kind in (0, 1, 3):
            free(kind, 0)
        free(2, n)

        @pl.loop(0, d_model // 256)
        def _(c):
            cols = pl.ds(pl.multiple_of(c * 256, 256), 256)
            hat[cols, :] = ha[:, cols].T
            hmt[cols, :] = hm[:, cols].T

        put_t(0, hat, o_ha, slot)
        put_t(1, hmt, o_hm, slot)
        pos = pl.ds(pl.multiple_of(base, rows), rows)
        cos_t, sin_t = cos_ref[pos, :], sin_ref[pos, :]

        @pl.loop(0, 4)
        def _(g):
            cols = pl.ds(pl.multiple_of(g * 384, 128), 384)
            t = dot_nn(ha[...], w2[:, cols]).astype(BF16)
            for j in range(2):
                v = t[:, j * 128:j * 128 + 128].astype(F32)
                qkv[s, :, pl.ds(pl.multiple_of(g * 384 + j * 128, 128), 128)] = (v * cos_t + pltpu.roll(v, 64, 1) * sin_t).astype(BF16)
            qkv[s, :, pl.ds(pl.multiple_of(g * 384 + 256, 128), 128)] = t[:, 256:384]

        put(2, n, qkv, o_qkv, slot)

    def up(slot, n):
        @pl.loop(0, 4)
        def _(c):
            cols = pl.ds(pl.multiple_of(c * 512, 512), 512)
            u = dot_nn(hm[...], wu[:, cols]).astype(BF16).astype(F32)
            cdf = 0.5 * (1.0 + lax.erf(u * (0.5 ** 0.5)))
            get[cols, :] = (u * cdf).astype(BF16).T
            slope[slot, :, cols] = cdf + u * (jnp.exp(-0.5 * u * u) * ((2.0 * jnp.pi) ** -0.5))

        put_t(3, get, o_gelu, slot)

    def down(slot, n):
        s = n % 2
        free(4, n)
        free(5, n)
        dc[s] = dot_nt(dy_v[slot], wo[...]).astype(BF16)
        put(5, n, dc, o_dctx, slot)

        @pl.loop(0, 4)
        def _(c):
            cols = pl.ds(pl.multiple_of(c * 512, 512), 512)
            d_gelu = dot_nt(dy_v[slot], wd[cols, :]).astype(BF16).astype(F32)
            dh[s, :, cols] = (d_gelu * slope[slot, :, cols]).astype(BF16)

        put(4, n, dh, o_dhid, slot)

    fins = []

    def keep(buf, ref, slot, i):
        copy = pltpu.make_async_copy(buf.at[slot], ref.at[pl.ds(pl.multiple_of(slot * rows, rows), rows)], fin_sem.at[i])
        copy.start()
        fins.append(copy)

    loads[0].wait()
    forward(tp, 0)
    loads[2].wait()
    up(tp, 0)
    keep(x_v, o_x, tp, 0)
    xm[0].wait_recv()
    xm[4].start()
    xm[1].wait_recv()
    xm[5].start()
    for i in range(4):
        dm[i].start()
    loads[1].wait()
    loads[3].wait()
    loads[4].wait()
    down(tp, 0)
    keep(dy_v, o_dy, tp, 4)
    xm[2].wait_recv()
    forward(prv, 1)
    up(prv, 1)
    keep(x_v, o_x, prv, 1)
    xm[3].wait_recv()
    forward(nxt, 2)
    up(nxt, 2)
    keep(x_v, o_x, nxt, 2)
    dm[0].wait_recv()
    dm[4].start()
    dm[1].wait_recv()
    dm[5].start()
    xm[4].wait_recv()
    xm[5].wait_recv()
    forward(opp, 3)
    up(opp, 3)
    keep(x_v, o_x, opp, 3)
    dm[2].wait_recv()
    down(prv, 1)
    keep(dy_v, o_dy, prv, 5)
    dm[3].wait_recv()
    down(nxt, 2)
    keep(dy_v, o_dy, nxt, 6)
    dm[4].wait_recv()
    dm[5].wait_recv()
    down(opp, 3)
    keep(dy_v, o_dy, opp, 7)
    for m in xm + dm:
        m.wait_send()
    for copy in list(outs.values()) + fins + [w_out_copy]:
        copy.wait()


def front_call(x_loc, dy_loc, ln_params, cos_f, sin_f, w_rows, w_up, w_down, w_out):
    r, d = x_loc.shape
    t, f, n, m = 4 * r, w_up.shape[1], w_rows.shape[0] * 128 // d, w_out.shape[0]
    part = w_rows.shape[0] // 4
    hbm = pl.BlockSpec(memory_space=pl.ANY)
    vmem = pl.BlockSpec(memory_space=pltpu.VMEM)
    dma = pltpu.SemaphoreType.DMA
    shape = jax.ShapeDtypeStruct
    return pl.pallas_call(
        front_kernel,
        in_specs=[hbm, hbm, vmem, vmem, vmem, hbm, hbm, hbm, hbm],
        out_specs=[hbm] * 9 + [vmem] * 2,
        out_shape=[shape((t, d), BF16)] * 2 + [shape((d, t), BF16)] * 2 + [
            shape((t, n), BF16), shape((f, t), BF16), shape((t, f), BF16), shape((t, m), BF16), shape((d, n), BF16),
            shape((t, 1), F32), shape((t, 1), F32)],
        scratch_shapes=[
            pltpu.VMEM((4, r, d), BF16), pltpu.VMEM((4, r, d), BF16),
            pltpu.VMEM((d, n), BF16), pltpu.VMEM((d, f), BF16), pltpu.VMEM((f, d), BF16), pltpu.VMEM((m, d), BF16),
            pltpu.VMEM((2, part, 128), BF16), pltpu.VMEM((part, 128), F32),
            pltpu.VMEM((4, r, f), F32),
            pltpu.VMEM((r, d), BF16), pltpu.VMEM((r, d), BF16),
            pltpu.VMEM((d, r), BF16), pltpu.VMEM((d, r), BF16), pltpu.VMEM((f, r), BF16),
            pltpu.VMEM((2, r, n), BF16), pltpu.VMEM((2, r, f), BF16), pltpu.VMEM((2, r, m), BF16),
            dma((6,)), dma((6,)), dma((6,)), dma((6,)), dma((5,)), dma((2,)), dma((6, 2)), dma((9,)),
        ],
        compiler_params=pltpu.CompilerParams(collective_id=1, has_side_effects=True, vmem_limit_bytes=64000 * 1024),
        cost_estimate=pl.CostEstimate(flops=2 * t * d * (n + 2 * f), bytes_accessed=70_000_000, transcendentals=2 * t * f),
        name='front',
    )(x_loc, dy_loc, ln_params, cos_f, sin_f, w_rows, w_up, w_down, w_out)


def back_kernel(get_ref, hmt_ref, hat_ref, dy_ref, dhid_ref, qkv_ref, dctx_ref, w2_ref, wup_ref, x_ref, xloc_ref, dyloc_ref,
                ln_ref, mean_ref, rstd_ref, cos_ref, sin_ref,
                o_gx, o_ln, o_qkv, o_out, o_up, o_down,
                a_buf, b_buf, p_buf, d_buf, l1, f1, l2, f2, lnb, dh_v, dproj_v, ctxt, qkv_b, dctx_b, dk_s, dv_s,
                wq_t, wu_t, x_t, c_buf, cl1, cf1, c_loc,
                a_sem, b_sem, dh_sem, h_sem, t_sem, g_sem, ds, dr, s_l1, r_l1, s_f1, r_f1, s_l2, r_l2, s_f2, r_f2, ln_s, ln_r,
                cs_l1, cr_l1, cs_f1, cr_f1, credit):
    tp = lax.axis_index('tp')
    dp = lax.axis_index('dp')
    core = lax.rem(dp, 2)
    y = lax.rem(dp // 2, 4)
    z = dp // 8
    partner = {'dp': dp + 1 - 2 * core}
    n_head = 4
    hd = 128
    blk = 256
    scale = hd ** -0.5

    def dev_y(i):
        return {'dp': z * 8 + i * 2 + core}

    def dev_z(i):
        return {'dp': i * 8 + y * 2 + core}

    def dev_x(i):
        return {'tp': i}

    def ring(i, d):
        return lax.rem(i + d, 4)

    def al(i, m):
        return pl.multiple_of(i * m, m)

    barrier = pltpu.get_barrier_semaphore()
    peers = [partner]
    for d in (1, 2, 3):
        peers += [dev_x(ring(tp, d)), dev_y(ring(y, d)), dev_z(ring(z, d))]
    for peer in peers:
        pl.semaphore_signal(barrier, inc=1, device_id=peer, device_id_type=MESH)

    def load_a(src, slot):
        return [pltpu.make_async_copy(src.at[pl.ds(1024 * w, 1024)], a_buf.at[slot, w], a_sem.at[slot, w]) for w in range(2)]

    def load_dy():
        return [pltpu.make_async_copy(dy_ref.at[:, pl.ds(1024 * w, 1024)], a_buf.at[1, w], a_sem.at[1, w]) for w in range(2)]

    def load_last():
        out = []
        for w in range(2):
            for i, src in enumerate((xloc_ref, dyloc_ref)):
                out.append(pltpu.make_async_copy(src.at[:, pl.ds(1024 * w, 1024)], a_buf.at[0, w, pl.ds(256 * i, 256)], g_sem.at[w, i]))
        return out

    def load_b(p, slot):
        return pltpu.make_async_copy(dy_ref.at[:, pl.ds(al(p, 256), 256)], b_buf.at[slot], b_sem.at[slot])

    def load_head(h, slot):
        return [pltpu.make_async_copy(qkv_ref.at[:, pl.ds(pl.multiple_of(h * 384, 128), 384)], qkv_b.at[slot], h_sem.at[slot, 0]),
                pltpu.make_async_copy(dctx_ref.at[:, pl.ds(al(h, 128), 128)], dctx_b.at[slot], h_sem.at[slot, 1])]

    def load_t(u, slot):
        at = pl.ds(al(u, 256), 256)
        return [pltpu.make_async_copy(w2_ref.at[at], wq_t.at[slot], t_sem.at[slot, 0]),
                pltpu.make_async_copy(wup_ref.at[at], wu_t.at[slot], t_sem.at[slot, 1]),
                pltpu.make_async_copy(x_ref.at[:, at], x_t.at[slot], t_sem.at[slot, 2])]

    def start(copies):
        for copy in copies:
            copy.start()

    def wait(copies):
        for copy in copies:
            copy.wait()

    start(load_a(get_ref, 0))
    load_b(jnp.int32(0), 0).start()
    start(load_head(jnp.int32(0), 0))
    start(load_a(hmt_ref, 1))
    dh_load = pltpu.make_async_copy(dhid_ref, dh_v, dh_sem)
    dh_load.start()
    pl.semaphore_wait(barrier, len(peers))

    def remote(src, dst, ssem, rsem, device):
        return pltpu.make_async_remote_copy(src_ref=src, dst_ref=dst, send_sem=ssem, recv_sem=rsem, device_id=device, device_id_type=MESH)

    def drain(ref, sem):
        pltpu.make_async_copy(ref, ref, sem).wait()

    def pair_copy(p):
        slot = lax.rem(p, SLOTS)
        return remote(p_buf.at[lax.rem(p, 2), :, :, :, 1 - core], d_buf.at[slot], ds.at[slot], dr.at[slot], partner)

    def blk1(slot, col, i, half):
        rows = pl.ds(32 * half, 32)
        if col == 0:
            return d_buf.at[slot, 0, :, i, rows, :]
        return d_buf.at[slot, 1, i, :, rows, :]

    def blk2(slot, col, i, half):
        rows = pl.ds(32 * half, 32)
        if col == 0:
            return d_buf.at[slot, 0, i, y, rows, :]
        return d_buf.at[slot, 1, z, i, rows, :]

    me1 = (y, z)
    dev1 = (dev_y, dev_z)
    me2 = (z, y)
    dev2 = (dev_z, dev_y)

    def compute(p):
        ps = lax.rem(p, 2)

        @pl.when(p >= 2)
        def _():
            drain(p_buf.at[ps, :, :, :, 0], ds.at[lax.rem(p - 2, SLOTS)])

        @pl.when(p < 7)
        def _():
            load_b(p + 1, 1 - ps).start()

        @pl.when((p == 0) | (p == 16))
        def _():
            wait(load_a(get_ref, 0))

        @pl.when((p == 8) | (p == 22))
        def _():
            wait(load_a(get_ref, 1))

        @pl.when(p < 8)
        def _():
            load_b(p, ps).wait()

        @pl.when(p == 8)
        def _():
            dh_load.wait()

        @pl.when((p >= 8) & (p < 16))
        def _():
            b_buf[ps] = dh_v[:, pl.ds(al(p - 8, 256), 256)]

        @pl.when((p >= 16) & (p < 22))
        def _():
            b_buf[ps] = dproj_v[:, pl.ds(al(p - 16, 256), 256)]

        @pl.when(p < 22)
        def _():
            sa = lax.rem(p // 8, 2)

            @pl.loop(0, 2)
            def _(h):
                tile = dot_nn(a_buf[sa, h], b_buf[ps])
                for i in range(16):
                    for col in range(2):
                        p_buf[ps, col, 2 * h + i // 8, (i // 2) % 4, i % 2] = tile[64 * i:64 * i + 64, 128 * col:128 * col + 128]

        @pl.when(p >= 22)
        def _():
            @pl.loop(0, 4)
            def _(k):
                tile = dot_nn(ctxt[...], a_buf[1, p - 22, :, pl.ds(al(k, 256), 256)])
                for i in range(32):
                    for col in range(2):
                        p_buf[ps, col, i // 8, (i // 2) % 4, i % 2, pl.ds(al(k, 16), 16), :] = tile[16 * i:16 * i + 16, 128 * col:128 * col + 128]

        @pl.when(p == 7)
        def _():
            start(load_a(hat_ref, 0))

        @pl.when(p == 15)
        def _():
            start(load_dy())

        @pl.when(p == 21)
        def _():
            start(load_last())

        @pl.when(p >= SLOTS)
        def _():
            pl.semaphore_wait(credit.at[0], 1)

        pair_copy(p).start()

    def first(blk, slot, me, dev, lands, finals, s_a, r_a, s_b, r_b):
        for col in range(2):
            nxt, opp, prv = ring(me[col], 1), ring(me[col], 2), ring(me[col], 3)
            remote(blk(slot, col, opp, 0), lands.at[slot, col, 0], s_a.at[slot], r_a.at[slot], dev[col](nxt)).start()
            remote(blk(slot, col, opp, 1), lands.at[slot, col, 1], s_a.at[slot], r_a.at[slot], dev[col](prv)).start()
        for col in range(2):
            nxt, prv = ring(me[col], 1), ring(me[col], 3)
            remote(blk(slot, col, nxt, 1), finals.at[slot, col, 0, 1], s_b.at[slot], r_b.at[slot], dev[col](nxt)).start()
            remote(blk(slot, col, prv, 0), finals.at[slot, col, 0, 0], s_b.at[slot], r_b.at[slot], dev[col](prv)).start()

    def second(blk, slot, me, dev, lands, finals, r_a, s_b, r_b):
        drain(lands.at[slot], r_a.at[slot])
        for col in range(2):
            nxt, prv = ring(me[col], 1), ring(me[col], 3)
            for half, to in ((0, nxt), (1, prv)):
                ref = blk(slot, col, to, half)
                ref[...] = ref[...] + lands[slot, col, half]
                remote(ref, finals.at[slot, col, 1, half], s_b.at[slot], r_b.at[slot], dev[col](to)).start()

    def stage_s(q):
        slot = lax.rem(q, SLOTS)
        ps = lax.rem(q, 2)
        drain(d_buf.at[slot], dr.at[slot])

        @pl.loop(0, 32)
        def _(i):
            col, zi, yi = i // 16, lax.rem(i // 4, 4), lax.rem(i, 4)
            d_buf[slot, col, zi, yi] = d_buf[slot, col, zi, yi] + p_buf[ps, col, zi, yi, core]

        @pl.when(q >= SLOTS)
        def _():
            for i in range(1, 5):
                pl.semaphore_wait(credit.at[i], 1)

        first(blk1, slot, me1, dev1, l1, f1, s_l1, r_l1, s_f1, r_f1)

    def stage_l1(q):
        second(blk1, lax.rem(q, SLOTS), me1, dev1, l1, f1, r_l1, s_f1, r_f1)

    def stage_f1(q):
        slot = lax.rem(q, SLOTS)
        drain(f1.at[slot], r_f1.at[slot])
        for col in range(2):
            for half in range(2):
                ref = blk1(slot, col, me1[col], half)
                ref[...] = ref[...] + (f1[slot, col, 0, half] + f1[slot, col, 1, half])
        first(blk2, slot, me2, dev2, l2, f2, s_l2, r_l2, s_f2, r_f2)

    def stage_l2(q):
        second(blk2, lax.rem(q, SLOTS), me2, dev2, l2, f2, r_l2, s_f2, r_f2)

    def stage_f2(q):
        slot = lax.rem(q, SLOTS)
        drain(f2.at[slot], r_f2.at[slot])
        for col in range(2):
            for half in range(2):
                rows = pl.ds(32 * half, 32)
                val = blk2(slot, col, me2[col], half)[...] + (f2[slot, col, 0, half] + f2[slot, col, 1, half])
                for out, lo, hi in ((o_down, 0, 8), (o_up, 8, 16), (o_qkv, 16, 22)):
                    @pl.when((q >= lo) & (q < hi))
                    def _():
                        out[rows, pl.ds(pl.multiple_of((q - lo) * 256 + col * 128, 128), 128)] = val

                @pl.when(q >= 22)
                def _():
                    for k in range(2):
                        at = (q - 22) * 1024 + (2 * half + k) * 256 + col * 128
                        o_out[:, pl.ds(pl.multiple_of(at, 128), 128)] = val[16 * k:16 * k + 16, :]
        drain(l1.at[slot], s_l1.at[slot])
        drain(f1.at[slot], s_f1.at[slot])
        drain(l2.at[slot], s_l2.at[slot])
        drain(f2.at[slot], s_f2.at[slot])

        @pl.when(q < PIECES - SLOTS)
        def _():
            to = (partner, dev_y(ring(y, 1)), dev_y(ring(y, 3)), dev_z(ring(z, 1)), dev_z(ring(z, 3)))
            for i in range(5):
                pl.semaphore_signal(credit.at[i], inc=1, device_id=to[i], device_id_type=MESH)

    def ln_send(stage):
        me, dev, n = ((core, None, 2), (tp, dev_x, 4), (y, dev_y, 4), (z, dev_z, 4))[stage]
        for d in range(1, n):
            to = partner if dev is None else dev(ring(me, d))
            remote(lnb.at[stage, me], lnb.at[stage, me], ln_s.at[stage], ln_r.at[stage], to).start()

    def ln_sum(stage):
        n = 2 if stage == 0 else 4
        ref = lnb.at[stage, pl.ds(0, n - 1)]
        drain(ref, ln_r.at[stage])
        drain(ref, ln_s.at[stage])
        if n == 2:
            return lnb[0, 0] + lnb[0, 1]
        return (lnb[stage, 0] + lnb[stage, 1]) + (lnb[stage, 2] + lnb[stage, 3])

    def unrope(d, rows):
        d = d.astype(BF16).astype(F32)
        return (d * cos_ref[rows, :] - pltpu.roll(d, hd // 2, 1) * sin_ref[rows, :]).astype(BF16)

    def attend(h, i):
        hs = lax.rem(h, 2)
        if i == 0:
            wait(load_head(h, hs))

            @pl.when(h < n_head - 1)
            def _():
                start(load_head(h + 1, 1 - hs))

        rows, n = slice(i * blk, (i + 1) * blk), (i + 1) * blk
        qi, dci = qkv_b[hs, rows, 0:hd], dctx_b[hs, rows, :]
        kn, vn = qkv_b[hs, :n, hd:2 * hd], qkv_b[hs, :n, 2 * hd:3 * hd]
        s = dot_nt(qi, kn) * scale
        row_id = lax.broadcasted_iota(jnp.int32, (blk, n), 0) + i * blk
        col_id = lax.broadcasted_iota(jnp.int32, (blk, n), 1)
        s = jnp.where(row_id >= col_id, s, -1e30)
        e = jnp.exp(s - jnp.max(s, axis=1, keepdims=True))
        p = e / jnp.sum(e, axis=1, keepdims=True)
        pb = p.astype(BF16)
        ctxt[pl.ds(al(h, hd), hd), rows] = dot_nn(pb, vn).astype(BF16).T
        dp_ = dot_nt(dci, vn).astype(BF16).astype(F32)
        dsb = (p * (dp_ - jnp.sum(p * dp_, axis=1, keepdims=True)) * scale).astype(BF16)

        def cols(j):
            return pl.ds(pl.multiple_of(h * 384 + j * 128, 128), 128)

        dproj_v[rows, cols(0)] = unrope(dot_nn(dsb, kn), rows)
        dk, dv = dot_tt(dsb, qi), dot_tt(pb, dci)
        lo = n - blk
        dk_s[lo:n, :] = dk[lo:, :]
        dv_s[lo:n, :] = dv[lo:, :]
        if lo:
            dk_s[:lo, :] = dk_s[:lo, :] + dk[:lo, :]
            dv_s[:lo, :] = dv_s[:lo, :] + dv[:lo, :]
        if i == 3:
            @pl.loop(0, 4)
            def _(m):
                at = pl.ds(al(m, blk), blk)
                dproj_v[at, cols(1)] = unrope(dk_s[at, :], at)
                dproj_v[at, cols(2)] = dv_s[at, :].astype(BF16)

    def inputs(u):
        us = lax.rem(u, 2)
        cs = lax.rem(u, 5)
        wait(load_t(u, us))

        @pl.when(u < 7)
        def _():
            start(load_t(u + 1, 1 - us))

        at = pl.ds(al(u, 256), 256)
        gain_a, gain_m = ln_ref[0:1, at], ln_ref[2:3, at]
        sums = []
        for m in range(2):
            rows = slice(512 * m, 512 * m + 512)
            dha = dot_nt(dproj_v[rows, :], wq_t[us]).astype(BF16).astype(F32)
            dhm = dot_nt(dh_v[rows, :], wu_t[us]).astype(BF16).astype(F32)
            x_hat = (x_t[us, rows, :].astype(F32) - mean_ref[rows, :]) * rstd_ref[rows, :]
            c = (dha * gain_a + dhm * gain_m).astype(BF16)
            c_buf[cs, 2 * m] = c[:256]
            c_buf[cs, 2 * m + 1] = c[256:]
            sums.append([jnp.sum(v, axis=0, keepdims=True) for v in (dha * x_hat, dha, dhm * x_hat, dhm)])
        for i in range(4):
            lnb[0, core, i:i + 1, at] = sums[0][i] + sums[1][i]
        nxt, opp, prv = ring(tp, 1), ring(tp, 2), ring(tp, 3)
        remote(c_blk(u, opp, 0), cl1.at[u, 0], cs_l1.at[u], cr_l1.at[u], dev_x(nxt)).start()
        remote(c_blk(u, opp, 1), cl1.at[u, 1], cs_l1.at[u], cr_l1.at[u], dev_x(prv)).start()
        remote(c_blk(u, nxt, 1), cf1.at[u, 0, 1], cs_f1.at[u], cr_f1.at[u], dev_x(nxt)).start()
        remote(c_blk(u, prv, 0), cf1.at[u, 0, 0], cs_f1.at[u], cr_f1.at[u], dev_x(prv)).start()

    def c_blk(u, i, half):
        return c_buf.at[lax.rem(u, 5), i, pl.ds(128 * half, 128), :]

    def c_second(u):
        drain(cl1.at[u], cr_l1.at[u])
        for half, to in ((0, ring(tp, 1)), (1, ring(tp, 3))):
            ref = c_blk(u, to, half)
            ref[...] = (ref[...].astype(F32) + cl1[u, half].astype(F32)).astype(BF16)
            remote(ref, cf1.at[u, 1, half], cs_f1.at[u], cr_f1.at[u], dev_x(to)).start()

    def c_final(u):
        drain(cf1.at[u], cr_f1.at[u])
        for half in range(2):
            c_loc[128 * half:128 * half + 128, pl.ds(al(u, 256), 256)] = c_blk(u, tp, half)[...].astype(F32) + (
                cf1[u, 0, half].astype(F32) + cf1[u, 1, half].astype(F32))
        drain(cl1.at[u], cs_l1.at[u])
        drain(cf1.at[u], cs_f1.at[u])

    def last():
        wait(load_last())

        @pl.loop(0, 8)
        def _(r):
            at = pl.ds(al(r, 32), 32)
            dy_at = pl.ds(pl.multiple_of(256 + r * 32, 32), 32)
            own = pl.ds(pl.multiple_of(tp * 256 + r * 32, 32), 32)
            mean, rstd = mean_ref[own, :], rstd_ref[own, :]
            c = c_loc[at, :]
            x_hat = (jnp.concatenate([a_buf[0, 0, at, :], a_buf[0, 1, at, :]], axis=1).astype(F32) - mean) * rstd
            dy_own = jnp.concatenate([a_buf[0, 0, dy_at, :], a_buf[0, 1, dy_at, :]], axis=1).astype(F32)
            dx = rstd * (c - jnp.mean(c, axis=-1, keepdims=True) - x_hat * jnp.mean(c * x_hat, axis=-1, keepdims=True))
            o_gx[at, :] = (dy_own + dx).astype(BF16)

    @pl.loop(0, STEPS)
    def _(p):
        @pl.when(p < PIECES)
        def _():
            compute(p)

        for lag, stage in ((7, stage_f2), (6, stage_l2), (5, stage_f1), (3, stage_l1), (1, stage_s)):
            @pl.when((p >= lag) & (p < PIECES + lag))
            def _():
                stage(p - lag)

        @pl.when((p >= 20) & (p < 28))
        def _():
            c_final(p - 20)

        @pl.when((p >= 18) & (p < 26))
        def _():
            c_second(p - 18)

        for i in range(4):
            @pl.when((p < 16) & (lax.rem(p, 4) == i))
            def _():
                attend(p // 4, i)

        @pl.when(p == 14)
        def _():
            start(load_t(0, 0))

        @pl.when((p >= 16) & (p < 24))
        def _():
            inputs(p - 16)

        @pl.when(p == 24)
        def _():
            ln_send(0)

        for stage, me in ((1, tp), (2, y), (3, z)):
            @pl.when(p == 24 + stage)
            def _():
                lnb[stage, me] = ln_sum(stage - 1)
                ln_send(stage)

        @pl.when(p == 28)
        def _():
            last()

        @pl.when(p == 29)
        def _():
            o_ln[...] = ln_sum(3)

    for p in (PIECES - 2, PIECES - 1):
        drain(p_buf.at[p % 2, :, :, :, 0], ds.at[p % SLOTS])


def back_call(get, hmt, hat, dy_full, d_hidden, qkv, d_ctx, w2, w_up, x_full, x_loc, dy_loc, ln_params, mean, rstd, cos_f, sin_f):
    hbm = pl.BlockSpec(memory_space=pl.ANY)
    vmem = pl.BlockSpec(memory_space=pltpu.VMEM)
    dma = pltpu.SemaphoreType.DMA
    shape = jax.ShapeDtypeStruct
    k = (SLOTS,)
    return pl.pallas_call(
        back_kernel,
        in_specs=[hbm] * 12 + [vmem] * 5,
        out_specs=[vmem] * 6,
        out_shape=[shape((256, 2048), BF16), shape((4, 2048), F32), shape((64, 1536), F32), shape((16, 2048), F32),
                   shape((64, 2048), F32), shape((64, 2048), F32)],
        scratch_shapes=[
            pltpu.VMEM((2, 2, 1024, 1024), BF16), pltpu.VMEM((2, 1024, 256), BF16),
            pltpu.VMEM((2, 2, 4, 4, 2, 64, 128), F32), pltpu.VMEM(k + (2, 4, 4, 64, 128), F32),
            pltpu.VMEM(k + (2, 2, 4, 32, 128), F32), pltpu.VMEM(k + (2, 2, 2, 4, 32, 128), F32),
            pltpu.VMEM(k + (2, 2, 32, 128), F32), pltpu.VMEM(k + (2, 2, 2, 32, 128), F32),
            pltpu.VMEM((4, 4, 4, 2048), F32),
            pltpu.VMEM((1024, 2048), BF16), pltpu.VMEM((1024, 1536), BF16), pltpu.VMEM((512, 1024), BF16),
            pltpu.VMEM((2, 1024, 384), BF16), pltpu.VMEM((2, 1024, 128), BF16),
            pltpu.VMEM((1024, 128), F32), pltpu.VMEM((1024, 128), F32),
            pltpu.VMEM((2, 256, 1536), BF16), pltpu.VMEM((2, 256, 2048), BF16), pltpu.VMEM((2, 1024, 256), BF16),
            pltpu.VMEM((5, 4, 256, 256), BF16), pltpu.VMEM((8, 2, 128, 256), BF16), pltpu.VMEM((8, 2, 2, 128, 256), BF16),
            pltpu.VMEM((256, 2048), F32),
            dma((2, 2)), dma((2,)), dma, dma((2, 2)), dma((2, 3)), dma((2, 2)),
            dma(k), dma(k), dma(k), dma(k), dma(k), dma(k), dma(k), dma(k), dma(k), dma(k),
            dma((4,)), dma((4,)), dma((8,)), dma((8,)), dma((8,)), dma((8,)),
            pltpu.SemaphoreType.REGULAR((5,)),
        ],
        compiler_params=pltpu.CompilerParams(collective_id=0, has_side_effects=True, vmem_limit_bytes=65400 * 1024),
        cost_estimate=pl.CostEstimate(flops=50_000_000_000, bytes_accessed=100_000_000, transcendentals=0),
        name='back',
    )(get, hmt, hat, dy_full, d_hidden, qkv, d_ctx, w2, w_up, x_full, x_loc, dy_loc, ln_params, mean, rstd, cos_f, sin_f)


def solution(mesh):
    def local_step(x_loc, dy_loc, ln_params, w_qkv, w_out, w_up, w_down):
        width, groups, slots, head_dim = w_qkv.shape
        cos_f, sin_f = (jnp.asarray(t) for t in rope_tables(4 * x_loc.shape[1], head_dim))
        w_rows = w_qkv.transpose(0, 2, 1, 3).reshape(width * slots * groups, head_dim)
        x_full, dy_full, hat, hmt, qkv, get, d_hidden, d_ctx, w2, mean, rstd = front_call(
            x_loc[0], dy_loc[0], ln_params, cos_f, sin_f, w_rows, w_up, w_down, w_out)
        grad_x, g_ln, g_qkv, g_out, g_up, g_down = back_call(
            get, hmt, hat, dy_full, d_hidden, qkv, d_ctx, w2, w_up, x_full, x_loc[0], dy_loc[0], ln_params, mean, rstd, cos_f, sin_f)
        return grad_x[None], g_ln, g_qkv.reshape(64, groups, slots, head_dim), g_out, g_up, g_down

    act_spec = P('dp', 'tp', None)
    in_specs = (act_spec, act_spec, P(None, None), P(None, 'tp', None, None), P('tp', None), P(None, 'tp'), P('tp', None))
    out_specs = (act_spec, P(None, None), P('dp', 'tp', None, None), P(('tp', 'dp'), None), P('dp', 'tp'), P(('tp', 'dp'), None))
    return jax.shard_map(local_step, mesh=mesh, in_specs=in_specs, out_specs=out_specs, check_vma=False)
```

time: 732 us -> 243 us (0.33); the launches traced: 723 us -> 243 us
  waiting for transfers between devices: 403 us -> 0 us
  Pallas kernels: 0 us -> 233 us
  matrix products: 192 us -> 0 us
  blocking collectives: 66.2 us -> 0 us
  other arithmetic: 26.4 us -> 0 us
  between operations: 15 us -> 0.67 us
  local copies, waits for them, and re-layouts: 20.2 us -> 9.05 us
    reduce_scatter x6 -> x0, waiting for transfers between devices: 341 us -> none  [the longest x1 119 us: local_step(): lax.psum_scatter(g_wdown, 'dp', scatter_dimension=0, tiled=True)]
    pallas_call x0 -> x2, Pallas kernels: none -> 233 us  [the longest x1 154 us: back_call(): pl.pallas_call(back_kernel, in_specs=[hbm] * 12 + [vmem] * 5, out_specs=[...]
    dot_general x15 -> x0, matrix products: 182 us -> none  [the longest x1 32.6 us: local_step(): jnp.einsum('btd,df->btf', h_mlp, w_up, preferred_element_type=jnp.float32)]
    psum x1 -> x0, blocking collectives: 66.2 us -> none  [local_step(): lax.psum(jnp.stack([dgain_attn, dshift_attn, dgain_mlp, dshift_mlp]), ('t...]
    all_gather x2 -> x0, waiting for transfers between devices: 60.1 us -> none  [the longest x1 37.2 us: local_step(): x_full = lax.all_gather(x_loc, 'tp', axis=1, tiled=True)]
    reduce_sum x6 -> x0, other arithmetic: 16.7 us -> none  [the longest x2 6.28 us: layer_norm(): centered * lax.rsqrt(row_var + NORM_EPS) * norm_gain + norm_shift]
    unnamed x54 -> x10, local copies, waits for them, and re-layouts: 18.7 us -> 7.69 us
    unnamed x1 -> x0, matrix products: 9.41 us -> none
  transfers between devices with their start and end apart: 8 -> 0, of which waited for: 6 -> 0; matrix products, arithmetic and copies ran while one was open for 24% -> 0% of each run, Pallas kernels for 0% -> 0%
where the time goes in v1:
time: 243 us
  Pallas kernels  233 us (96%)
  local copies, waits for them, and re-layouts  9.05 us (4%)
    pallas_call x1, Pallas kernels, back_call(): pl.pallas_call(back_kernel, in_specs=[hbm] * 12 + [vmem] * 5, out_specs=[...  154 us
    pallas_call x1, Pallas kernels, front_call(): pl.pallas_call(front_kernel, in_specs=[hbm, hbm, vmem, vmem, vmem, hbm, h...  79.3 us
    unnamed x10, local copies, waits for them, and re-layouts  7.69 us

profile of v1, /device:TPU:0, one launch (start us, length us, event | category | flops | bytes accessed | tf_op | source)
XLA Modules:
  0.0 242.8 jit_solution(17935995095277319597)
XLA Ops:
  0.6 79.3 %front.1 = (bf16[1024,2048]{1,0:T(8,128)(2,1)}, bf16[1024,2048]{1,0:T(8,128)(2,1)}, bf16[2048,1024]{1,0:T(8,128)(2,1)}, bf16[2048,1024]{1,0:T(8,128)(2,1)}, bf16...) custom-call(bf16[256,2048]{1,0:T(8,128)(2,1)} %bitcast.8, ...), custom_call_target="tpu_custom_call" | custom-call | flops 23622320128 | bytes 70000000 | tf_op jit(solution)/shard_map/front/pallas_call | solution.py:252
  79.9 153.8 %back.1 = (bf16[256,2048]{1,0:T(8,128)(2,1)}, f32[4,2048]{1,0:T(4,128)}, f32[64,1536]{1,0:T(8,128)}, f32[16,2048]{1,0:T(8,128)}, f32[64,2048]{1,0:T(8,128)}, /*index=5*/f32[64,2048]{1,0:T(8,128)}) custom-call(bf16[2048,1024]{1,0:T(8,128)(2,1)} %get-tuple-element.23.get_ref, bf16[2048,1024]{1,0:T(8,128)(2,1)} %get-tuple-element.24.hmt_ref, ...), custom_call_target="tpu_custom_call" | custom-call | flops 49999998976 | bytes 100000000 | tf_op jit(solution)/shard_map/back/pallas_call | solution.py:718
  233.7 0.0 copy-start.1
  233.7 0.0 copy-start
  233.7 1.4 reshape.19
  235.1 0.8 copy.16
  236.0 2.3 copy.22
  238.3 1.4 copy.23
  239.6 1.6 copy.24
  241.2 0.0 copy-done.1
  241.2 0.8 copy.25
  242.0 0.0 copy-done
  242.0 0.8 copy.26
Async XLA Ops:
  233.7 7.5 %copy-start.1 = (f32[64,2048]{1,0:T(8,128)S(1)}, f32[64,2048]{1,0:T(8,128)}, u32[]{:S(2)}) copy-start(f32[64,2048]{1,0:T(8,128)} %get-tuple-element.62) | copy-start | bytes 1572868
  233.7 8.3 %copy-start = (f32[64,2048]{1,0:T(8,128)S(1)}, f32[64,2048]{1,0:T(8,128)}, u32[]{:S(2)}) copy-start(f32[64,2048]{1,0:T(8,128)} %get-tuple-element.63) | copy-start | bytes 1572868

commit v2 on v1

--- a/solution.py
+++ b/solution.py
@@ -14,6 +14,8 @@
 PIECES = 24
 SLOTS = 8
 STEPS = PIECES + 7
+EARLY = 768
+LATE = 5
 F32 = jnp.float32
 BF16 = jnp.bfloat16
 
@@ -38,9 +40,9 @@
     return lax.dot_general(lhs, rhs, (((0,), (0,)), ((), ())), preferred_element_type=F32)
 
 
-def front_kernel(x_ref, dy_ref, ln_ref, cos_ref, sin_ref, wq_ref, wu_ref, wd_ref, wo_ref,
-                 o_x, o_dy, o_ha, o_hm, o_qkv, o_gelu, o_dhid, o_dctx, o_w, mean_ref, rstd_ref,
-                 x_v, dy_v, w2, wu, wd, wo, wq_b, wq_f, slope, ha, hm, hat, hmt, get, qkv, dh, dc,
+def front_kernel(x_ref, dy_ref, ln_ref, cos_ref, sin_ref, wq_ref, wu_ref,
+                 o_x, o_dy, o_ha, o_hm, o_qkv, o_gelu, o_slope, o_w, mean_ref, rstd_ref,
+                 x_v, dy_v, w2, wu, wq_b, wq_f, slope, ha, hm, hat, hmt, get, qkv,
                  xs, xr, ds, dr, in_sem, wq_sem, out_sem, fin_sem):
     tp = lax.axis_index('tp')
     nxt, opp, prv = lax.rem(tp + 1, 4), lax.rem(tp + 2, 4), lax.rem(tp + 3, 4)
@@ -55,16 +57,14 @@
     def wq_copy(i):
         return pltpu.make_async_copy(wq_ref.at[pl.ds(i * part, part)], wq_b.at[i % 2], wq_sem.at[i % 2])
 
-    loads = [pltpu.make_async_copy(x_ref, x_v.at[tp], in_sem.at[0]), pltpu.make_async_copy(dy_ref, dy_v.at[tp], in_sem.at[1]),
-             pltpu.make_async_copy(wu_ref, wu, in_sem.at[2]), pltpu.make_async_copy(wd_ref, wd, in_sem.at[3]),
-             pltpu.make_async_copy(wo_ref, wo, in_sem.at[4])]
+    dy_own = dy_ref.at[:, pl.ds(0, EARLY)]
+    loads = [pltpu.make_async_copy(x_ref, x_v.at[tp], in_sem.at[0]), pltpu.make_async_copy(dy_own, dy_v.at[tp], in_sem.at[1]),
+             pltpu.make_async_copy(wu_ref, wu, in_sem.at[2])]
     wq_copy(0).start()
     loads[0].start()
     wq_copy(1).start()
     loads[2].start()
     loads[1].start()
-    loads[3].start()
-    loads[4].start()
     pl.semaphore_wait(barrier, 2)
 
     A, B = pl.ds(0, half), pl.ds(half, half)
@@ -77,7 +77,7 @@
                 one(4, buf.at[prv, A], prv, A, nxt), one(5, buf.at[nxt, B], nxt, B, prv)]
 
     xm = moves(x_ref, x_v, xs, xr)
-    dm = moves(dy_ref, dy_v, ds, dr)
+    dm = moves(dy_own, dy_v, ds, dr)
     for i in range(4):
         xm[i].start()
 
@@ -100,42 +100,51 @@
 
     outs = {}
 
-    def start(kind, n, src, dst):
-        copy = pltpu.make_async_copy(src, dst, out_sem.at[kind, n % 2])
-        copy.start()
-        outs[kind, n % 2] = copy
-
-    def put(kind, n, buf, ref, slot):
-        start(kind, n, buf.at[n % 2], ref.at[pl.ds(pl.multiple_of(slot * rows, rows), rows)])
-
-    def put_t(kind, buf, ref, slot):
-        start(kind, 0, buf, ref.at[:, pl.ds(pl.multiple_of(slot * rows, rows), rows)])
+    def tokens(block, i):
+        slot, side = block[i]
+        return pl.ds(pl.multiple_of(slot * rows + side * half, half), half)
+
+    def put(kind, n, buf, ref, block):
+        for i in range(2):
+            copy = pltpu.make_async_copy(buf.at[n % 2, pl.ds(i * half, half)], ref.at[tokens(block, i)], out_sem.at[kind, n % 2, i])
+            copy.start()
+            outs[kind, n % 2, i] = copy
+
+    def put_t(kind, buf, ref, block):
+        for i in range(2):
+            copy = pltpu.make_async_copy(buf.at[:, pl.ds(i * half, half)], ref.at[:, tokens(block, i)], out_sem.at[kind, 0, i])
+            copy.start()
+            outs[kind, 0, i] = copy
 
     def free(kind, n):
-        if (kind, n % 2) in outs:
-            outs.pop((kind, n % 2)).wait()
-
-    def forward(slot, n):
+        for i in range(2):
+            if (kind, n % 2, i) in outs:
+                outs.pop((kind, n % 2, i)).wait()
+
+    def forward(block, n):
         s = n % 2
-        base = slot * rows
-
-        @pl.loop(0, rows // 32)
-        def _(r):
-            at = pl.ds(pl.multiple_of(r * 32, 32), 32)
-            to = pl.ds(pl.multiple_of(base + r * 32, 32), 32)
-            xf = x_v[slot, at, :].astype(F32)
-            mean = jnp.mean(xf, axis=-1, keepdims=True)
-            cen = xf - mean
-            rstd = lax.rsqrt(jnp.mean(cen * cen, axis=-1, keepdims=True) + NORM_EPS)
-            mean_ref[to, :] = mean
-            rstd_ref[to, :] = rstd
-            x_hat = cen * rstd
-            ha[at, :] = (x_hat * ln_ref[0:1, :] + ln_ref[1:2, :]).astype(BF16)
-            hm[at, :] = (x_hat * ln_ref[2:3, :] + ln_ref[3:4, :]).astype(BF16)
+        for i in range(2):
+            slot, side = block[i]
+
+            @pl.loop(0, half // 32)
+            def _(r):
+                src = pl.ds(pl.multiple_of(side * half + r * 32, 32), 32)
+                at = pl.ds(pl.multiple_of(i * half + r * 32, 32), 32)
+                to = pl.ds(pl.multiple_of(slot * rows + side * half + r * 32, 32), 32)
+                xf = x_v[slot, src, :].astype(F32)
+                mean = jnp.mean(xf, axis=-1, keepdims=True)
+                cen = xf - mean
+                rstd = lax.rsqrt(jnp.mean(cen * cen, axis=-1, keepdims=True) + NORM_EPS)
+                mean_ref[to, :] = mean
+                rstd_ref[to, :] = rstd
+                x_hat = cen * rstd
+                ha[at, :] = (x_hat * ln_ref[0:1, :] + ln_ref[1:2, :]).astype(BF16)
+                hm[at, :] = (x_hat * ln_ref[2:3, :] + ln_ref[3:4, :]).astype(BF16)
 
         for kind in (0, 1, 3):
             free(kind, 0)
         free(2, n)
+        free(4, n)
 
         @pl.loop(0, d_model // 256)
         def _(c):
@@ -143,10 +152,9 @@
             hat[cols, :] = ha[:, cols].T
             hmt[cols, :] = hm[:, cols].T
 
-        put_t(0, hat, o_ha, slot)
-        put_t(1, hmt, o_hm, slot)
-        pos = pl.ds(pl.multiple_of(base, rows), rows)
-        cos_t, sin_t = cos_ref[pos, :], sin_ref[pos, :]
+        put_t(0, hat, o_ha, block)
+        put_t(1, hmt, o_hm, block)
+        cos_t, sin_t = (jnp.concatenate([ref[tokens(block, 0), :], ref[tokens(block, 1), :]], axis=0) for ref in (cos_ref, sin_ref))
 
         @pl.loop(0, 4)
         def _(g):
@@ -157,33 +165,18 @@
                 qkv[s, :, pl.ds(pl.multiple_of(g * 384 + j * 128, 128), 128)] = (v * cos_t + pltpu.roll(v, 64, 1) * sin_t).astype(BF16)
             qkv[s, :, pl.ds(pl.multiple_of(g * 384 + 256, 128), 128)] = t[:, 256:384]
 
-        put(2, n, qkv, o_qkv, slot)
-
-    def up(slot, n):
+        put(2, n, qkv, o_qkv, block)
+
         @pl.loop(0, 4)
         def _(c):
             cols = pl.ds(pl.multiple_of(c * 512, 512), 512)
             u = dot_nn(hm[...], wu[:, cols]).astype(BF16).astype(F32)
             cdf = 0.5 * (1.0 + lax.erf(u * (0.5 ** 0.5)))
             get[cols, :] = (u * cdf).astype(BF16).T
-            slope[slot, :, cols] = cdf + u * (jnp.exp(-0.5 * u * u) * ((2.0 * jnp.pi) ** -0.5))
-
-        put_t(3, get, o_gelu, slot)
-
-    def down(slot, n):
-        s = n % 2
-        free(4, n)
-        free(5, n)
-        dc[s] = dot_nt(dy_v[slot], wo[...]).astype(BF16)
-        put(5, n, dc, o_dctx, slot)
-
-        @pl.loop(0, 4)
-        def _(c):
-            cols = pl.ds(pl.multiple_of(c * 512, 512), 512)
-            d_gelu = dot_nt(dy_v[slot], wd[cols, :]).astype(BF16).astype(F32)
-            dh[s, :, cols] = (d_gelu * slope[slot, :, cols]).astype(BF16)
-
-        put(4, n, dh, o_dhid, slot)
+            slope[s, :, cols] = cdf + u * (jnp.exp(-0.5 * u * u) * ((2.0 * jnp.pi) ** -0.5))
+
+        put_t(3, get, o_gelu, block)
+        put(4, n, slope, o_slope, block)
 
     fins = []
 
@@ -193,57 +186,43 @@
         fins.append(copy)
 
     loads[0].wait()
-    forward(tp, 0)
     loads[2].wait()
-    up(tp, 0)
     keep(x_v, o_x, tp, 0)
+    forward(((tp, 0), (tp, 1)), 0)
     xm[0].wait_recv()
     xm[4].start()
     xm[1].wait_recv()
     xm[5].start()
     for i in range(4):
         dm[i].start()
-    loads[1].wait()
-    loads[3].wait()
-    loads[4].wait()
-    down(tp, 0)
-    keep(dy_v, o_dy, tp, 4)
+    forward(((prv, 0), (nxt, 1)), 1)
     xm[2].wait_recv()
-    forward(prv, 1)
-    up(prv, 1)
+    xm[3].wait_recv()
     keep(x_v, o_x, prv, 1)
-    xm[3].wait_recv()
-    forward(nxt, 2)
-    up(nxt, 2)
     keep(x_v, o_x, nxt, 2)
+    forward(((prv, 1), (nxt, 0)), 2)
     dm[0].wait_recv()
     dm[4].start()
     dm[1].wait_recv()
     dm[5].start()
     xm[4].wait_recv()
     xm[5].wait_recv()
-    forward(opp, 3)
-    up(opp, 3)
     keep(x_v, o_x, opp, 3)
-    dm[2].wait_recv()
-    down(prv, 1)
-    keep(dy_v, o_dy, prv, 5)
-    dm[3].wait_recv()
-    down(nxt, 2)
-    keep(dy_v, o_dy, nxt, 6)
-    dm[4].wait_recv()
-    dm[5].wait_recv()
-    down(opp, 3)
-    keep(dy_v, o_dy, opp, 7)
+    forward(((opp, 0), (opp, 1)), 3)
+    loads[1].wait()
+    for i in range(2, 6):
+        dm[i].wait_recv()
+    for i, slot in enumerate((tp, prv, nxt, opp)):
+        keep(dy_v, o_dy, slot, 4 + i)
     for m in xm + dm:
         m.wait_send()
     for copy in list(outs.values()) + fins + [w_out_copy]:
         copy.wait()
 
 
-def front_call(x_loc, dy_loc, ln_params, cos_f, sin_f, w_rows, w_up, w_down, w_out):
+def front_call(x_loc, dy_loc, ln_params, cos_f, sin_f, w_rows, w_up):
     r, d = x_loc.shape
-    t, f, n, m = 4 * r, w_up.shape[1], w_rows.shape[0] * 128 // d, w_out.shape[0]
+    t, f, n = 4 * r, w_up.shape[1], w_rows.shape[0] * 128 // d
     part = w_rows.shape[0] // 4
     hbm = pl.BlockSpec(memory_space=pl.ANY)
     vmem = pl.BlockSpec(memory_space=pltpu.VMEM)
@@ -251,33 +230,33 @@
     shape = jax.ShapeDtypeStruct
     return pl.pallas_call(
         front_kernel,
-        in_specs=[hbm, hbm, vmem, vmem, vmem, hbm, hbm, hbm, hbm],
-        out_specs=[hbm] * 9 + [vmem] * 2,
-        out_shape=[shape((t, d), BF16)] * 2 + [shape((d, t), BF16)] * 2 + [
-            shape((t, n), BF16), shape((f, t), BF16), shape((t, f), BF16), shape((t, m), BF16), shape((d, n), BF16),
-            shape((t, 1), F32), shape((t, 1), F32)],
+        in_specs=[hbm, hbm, vmem, vmem, vmem, hbm, hbm],
+        out_specs=[hbm] * 8 + [vmem] * 2,
+        out_shape=[shape((t, d), BF16), shape((t, EARLY), BF16), shape((d, t), BF16), shape((d, t), BF16),
+                   shape((t, n), BF16), shape((f, t), BF16), shape((t, f), F32), shape((d, n), BF16),
+                   shape((t, 1), F32), shape((t, 1), F32)],
         scratch_shapes=[
-            pltpu.VMEM((4, r, d), BF16), pltpu.VMEM((4, r, d), BF16),
-            pltpu.VMEM((d, n), BF16), pltpu.VMEM((d, f), BF16), pltpu.VMEM((f, d), BF16), pltpu.VMEM((m, d), BF16),
+            pltpu.VMEM((4, r, d), BF16), pltpu.VMEM((4, r, EARLY), BF16),
+            pltpu.VMEM((d, n), BF16), pltpu.VMEM((d, f), BF16),
             pltpu.VMEM((2, part, 128), BF16), pltpu.VMEM((part, 128), F32),
-            pltpu.VMEM((4, r, f), F32),
+            pltpu.VMEM((2, r, f), F32),
             pltpu.VMEM((r, d), BF16), pltpu.VMEM((r, d), BF16),
             pltpu.VMEM((d, r), BF16), pltpu.VMEM((d, r), BF16), pltpu.VMEM((f, r), BF16),
-            pltpu.VMEM((2, r, n), BF16), pltpu.VMEM((2, r, f), BF16), pltpu.VMEM((2, r, m), BF16),
-            dma((6,)), dma((6,)), dma((6,)), dma((6,)), dma((5,)), dma((2,)), dma((6, 2)), dma((9,)),
+            pltpu.VMEM((2, r, n), BF16),
+            dma((6,)), dma((6,)), dma((6,)), dma((6,)), dma((3,)), dma((2,)), dma((5, 2, 2)), dma((9,)),
         ],
         compiler_params=pltpu.CompilerParams(collective_id=1, has_side_effects=True, vmem_limit_bytes=64000 * 1024),
-        cost_estimate=pl.CostEstimate(flops=2 * t * d * (n + 2 * f), bytes_accessed=70_000_000, transcendentals=2 * t * f),
+        cost_estimate=pl.CostEstimate(flops=2 * t * d * (n + f), bytes_accessed=70_000_000, transcendentals=2 * t * f),
         name='front',
-    )(x_loc, dy_loc, ln_params, cos_f, sin_f, w_rows, w_up, w_down, w_out)
-
-
-def back_kernel(get_ref, hmt_ref, hat_ref, dy_ref, dhid_ref, qkv_ref, dctx_ref, w2_ref, wup_ref, x_ref, xloc_ref, dyloc_ref,
+    )(x_loc, dy_loc, ln_params, cos_f, sin_f, w_rows, w_up)
+
+
+def back_kernel(get_ref, hmt_ref, hat_ref, dyp_ref, slope_ref, qkv_ref, wo_ref, wd_ref, w2_ref, wup_ref, x_ref, xloc_ref, dyloc_ref,
                 ln_ref, mean_ref, rstd_ref, cos_ref, sin_ref,
                 o_gx, o_ln, o_qkv, o_out, o_up, o_down,
                 a_buf, b_buf, p_buf, d_buf, l1, f1, l2, f2, lnb, dh_v, dproj_v, ctxt, qkv_b, dctx_b, dk_s, dv_s,
-                wq_t, wu_t, x_t, c_buf, cl1, cf1, c_loc,
-                a_sem, b_sem, dh_sem, h_sem, t_sem, g_sem, ds, dr, s_l1, r_l1, s_f1, r_f1, s_l2, r_l2, s_f2, r_f2, ln_s, ln_r,
+                wq_t, wu_t, x_t, c_buf, cl1, cf1, sl_buf, dy_v, wo_t,
+                a_sem, dy_sem, h_sem, t_sem, d_sem, g_sem, gs, gr, ds, dr, s_l1, r_l1, s_f1, r_f1, s_l2, r_l2, s_f2, r_f2, ln_s, ln_r,
                 cs_l1, cr_l1, cs_f1, cr_f1, credit):
     tp = lax.axis_index('tp')
     dp = lax.axis_index('dp')
@@ -312,25 +291,20 @@
     for peer in peers:
         pl.semaphore_signal(barrier, inc=1, device_id=peer, device_id_type=MESH)
 
-    def load_a(src, slot):
-        return [pltpu.make_async_copy(src.at[pl.ds(1024 * w, 1024)], a_buf.at[slot, w], a_sem.at[slot, w]) for w in range(2)]
-
-    def load_dy():
-        return [pltpu.make_async_copy(dy_ref.at[:, pl.ds(1024 * w, 1024)], a_buf.at[1, w], a_sem.at[1, w]) for w in range(2)]
-
-    def load_last():
-        out = []
-        for w in range(2):
-            for i, src in enumerate((xloc_ref, dyloc_ref)):
-                out.append(pltpu.make_async_copy(src.at[:, pl.ds(1024 * w, 1024)], a_buf.at[0, w, pl.ds(256 * i, 256)], g_sem.at[w, i]))
-        return out
-
-    def load_b(p, slot):
-        return pltpu.make_async_copy(dy_ref.at[:, pl.ds(al(p, 256), 256)], b_buf.at[slot], b_sem.at[slot])
+    def load_a(src, h):
+        return pltpu.make_async_copy(src.at[pl.ds(al(h, 1024), 1024)], a_buf.at[h], a_sem.at[h])
+
+    def load_x():
+        return [pltpu.make_async_copy(xloc_ref.at[:, pl.ds(256 * u, 256)], x_t.at[u // 4, pl.ds(256 * (u % 4), 256)], g_sem) for u in range(8)]
 
     def load_head(h, slot):
         return [pltpu.make_async_copy(qkv_ref.at[:, pl.ds(pl.multiple_of(h * 384, 128), 384)], qkv_b.at[slot], h_sem.at[slot, 0]),
-                pltpu.make_async_copy(dctx_ref.at[:, pl.ds(al(h, 128), 128)], dctx_b.at[slot], h_sem.at[slot, 1])]
+                pltpu.make_async_copy(wo_ref.at[pl.ds(al(h, 128), 128)], wo_t.at[slot], h_sem.at[slot, 1])]
+
+    def load_d(k, slot):
+        at = pl.ds(al(k, 256), 256)
+        return [pltpu.make_async_copy(wd_ref.at[at], wu_t.at[slot], d_sem.at[slot, 0]),
+                pltpu.make_async_copy(slope_ref.at[:, at], sl_buf.at[slot], d_sem.at[slot, 1])]
 
     def load_t(u, slot):
         at = pl.ds(al(u, 256), 256)
@@ -346,12 +320,15 @@
         for copy in copies:
             copy.wait()
 
-    start(load_a(get_ref, 0))
-    load_b(jnp.int32(0), 0).start()
+    for h in range(2):
+        load_a(get_ref, jnp.int32(h)).start()
+    early = pltpu.make_async_copy(dyp_ref, dy_v.at[:, pl.ds(0, EARLY)], dy_sem.at[0])
+    early.start()
+    late = pltpu.make_async_copy(dyloc_ref.at[:, pl.ds(EARLY, 256 * LATE)],
+                                 dy_v.at[pl.ds(al(tp, 256), 256), pl.ds(EARLY, 256 * LATE)], dy_sem.at[1])
+    late.start()
     start(load_head(jnp.int32(0), 0))
-    start(load_a(hmt_ref, 1))
-    dh_load = pltpu.make_async_copy(dhid_ref, dh_v, dh_sem)
-    dh_load.start()
+    start(load_d(jnp.int32(0), 0))
     pl.semaphore_wait(barrier, len(peers))
 
     def remote(src, dst, ssem, rsem, device):
@@ -359,6 +336,30 @@
 
     def drain(ref, sem):
         pltpu.make_async_copy(ref, ref, sem).wait()
+
+    def slice_copy(j, i):
+        cols = pl.ds(pl.multiple_of(EARLY + j * 256, 256), 256)
+        nxt, prv = ring(tp, 1), ring(tp, 3)
+        owner, half, to = ((tp, 0, nxt), (tp, 1, prv), (tp, 1, nxt), (tp, 0, prv), (prv, 0, nxt), (nxt, 1, prv))[i]
+        spot = dy_v.at[pl.ds(pl.multiple_of(owner * 256 + half * 128, 128), 128), cols]
+        src = dyloc_ref.at[pl.ds(128 * half, 128), cols] if i < 4 else spot
+        return remote(src, spot, gs.at[j, i], gr.at[j, i], dev_x(to))
+
+    def slice_own(j):
+        for i in range(4):
+            slice_copy(j, i).start()
+
+    def slice_on(j):
+        for i in range(2):
+            slice_copy(j, i).wait_recv()
+            slice_copy(j, 4 + i).start()
+
+    def slice_done(j):
+        for i in range(2, 6):
+            slice_copy(j, i).wait_recv()
+
+    slice_own(jnp.int32(0))
+    slice_own(jnp.int32(1))
 
     def pair_copy(p):
         slot = lax.rem(p, SLOTS)
@@ -388,25 +389,25 @@
         def _():
             drain(p_buf.at[ps, :, :, :, 0], ds.at[lax.rem(p - 2, SLOTS)])
 
-        @pl.when(p < 7)
-        def _():
-            load_b(p + 1, 1 - ps).start()
-
-        @pl.when((p == 0) | (p == 16))
-        def _():
-            wait(load_a(get_ref, 0))
-
-        @pl.when((p == 8) | (p == 22))
-        def _():
-            wait(load_a(get_ref, 1))
+        @pl.when(p == 0)
+        def _():
+            early.wait()
+
+        @pl.when(p == 3)
+        def _():
+            late.wait()
+
+        @pl.when((p >= 3) & (p < 7))
+        def _():
+            slice_done(p - 3)
+
+        @pl.when(p == 6)
+        def _():
+            slice_done(p - 2)
 
         @pl.when(p < 8)
         def _():
-            load_b(p, ps).wait()
-
-        @pl.when(p == 8)
-        def _():
-            dh_load.wait()
+            b_buf[ps] = dy_v[:, pl.ds(al(p, 256), 256)]
 
         @pl.when((p >= 8) & (p < 16))
         def _():
@@ -418,35 +419,33 @@
 
         @pl.when(p < 22)
         def _():
-            sa = lax.rem(p // 8, 2)
-
             @pl.loop(0, 2)
             def _(h):
-                tile = dot_nn(a_buf[sa, h], b_buf[ps])
+                @pl.when((p == 0) | (p == 8) | (p == 16))
+                def _():
+                    load_a(get_ref, h).wait()
+
+                tile = dot_nn(a_buf[h], b_buf[ps])
                 for i in range(16):
                     for col in range(2):
                         p_buf[ps, col, 2 * h + i // 8, (i // 2) % 4, i % 2] = tile[64 * i:64 * i + 64, 128 * col:128 * col + 128]
 
+                @pl.when(p == 7)
+                def _():
+                    load_a(hmt_ref, h).start()
+
+                @pl.when(p == 15)
+                def _():
+                    load_a(hat_ref, h).start()
+
         @pl.when(p >= 22)
         def _():
             @pl.loop(0, 4)
             def _(k):
-                tile = dot_nn(ctxt[...], a_buf[1, p - 22, :, pl.ds(al(k, 256), 256)])
+                tile = dot_nn(ctxt[...], dy_v[:, pl.ds(pl.multiple_of((p - 22) * 1024 + k * 256, 256), 256)])
                 for i in range(32):
                     for col in range(2):
                         p_buf[ps, col, i // 8, (i // 2) % 4, i % 2, pl.ds(al(k, 16), 16), :] = tile[16 * i:16 * i + 16, 128 * col:128 * col + 128]
-
-        @pl.when(p == 7)
-        def _():
-            start(load_a(hat_ref, 0))
-
-        @pl.when(p == 15)
-        def _():
-            start(load_dy())
-
-        @pl.when(p == 21)
-        def _():
-            start(load_last())
 
         @pl.when(p >= SLOTS)
         def _():
@@ -552,46 +551,57 @@
         d = d.astype(BF16).astype(F32)
         return (d * cos_ref[rows, :] - pltpu.roll(d, hd // 2, 1) * sin_ref[rows, :]).astype(BF16)
 
-    def attend(h, i):
+    def attend(h, side):
         hs = lax.rem(h, 2)
-        if i == 0:
+
+        def cols(j):
+            return pl.ds(pl.multiple_of(h * 384 + j * 128, 128), 128)
+
+        if side == 0:
             wait(load_head(h, hs))
 
             @pl.when(h < n_head - 1)
             def _():
                 start(load_head(h + 1, 1 - hs))
 
-        rows, n = slice(i * blk, (i + 1) * blk), (i + 1) * blk
-        qi, dci = qkv_b[hs, rows, 0:hd], dctx_b[hs, rows, :]
-        kn, vn = qkv_b[hs, :n, hd:2 * hd], qkv_b[hs, :n, 2 * hd:3 * hd]
-        s = dot_nt(qi, kn) * scale
-        row_id = lax.broadcasted_iota(jnp.int32, (blk, n), 0) + i * blk
-        col_id = lax.broadcasted_iota(jnp.int32, (blk, n), 1)
-        s = jnp.where(row_id >= col_id, s, -1e30)
-        e = jnp.exp(s - jnp.max(s, axis=1, keepdims=True))
-        p = e / jnp.sum(e, axis=1, keepdims=True)
-        pb = p.astype(BF16)
-        ctxt[pl.ds(al(h, hd), hd), rows] = dot_nn(pb, vn).astype(BF16).T
-        dp_ = dot_nt(dci, vn).astype(BF16).astype(F32)
-        dsb = (p * (dp_ - jnp.sum(p * dp_, axis=1, keepdims=True)) * scale).astype(BF16)
-
-        def cols(j):
-            return pl.ds(pl.multiple_of(h * 384 + j * 128, 128), 128)
-
-        dproj_v[rows, cols(0)] = unrope(dot_nn(dsb, kn), rows)
-        dk, dv = dot_tt(dsb, qi), dot_tt(pb, dci)
-        lo = n - blk
-        dk_s[lo:n, :] = dk[lo:, :]
-        dv_s[lo:n, :] = dv[lo:, :]
-        if lo:
-            dk_s[:lo, :] = dk_s[:lo, :] + dk[:lo, :]
-            dv_s[:lo, :] = dv_s[:lo, :] + dv[:lo, :]
-        if i == 3:
+            dctx_b[...] = dot_nt(dy_v[...], wo_t[hs]).astype(BF16)
+            dk_s[...] = jnp.zeros_like(dk_s)
+            dv_s[...] = jnp.zeros_like(dv_s)
+
+        for i in ((0, 3), (1, 2))[side]:
+            rows, lo, n = slice(i * blk, (i + 1) * blk), i * blk, (i + 1) * blk
+            qi, dci = qkv_b[hs, rows, 0:hd], dctx_b[rows, :]
+            kn, vn = qkv_b[hs, :n, hd:2 * hd], qkv_b[hs, :n, 2 * hd:3 * hd]
+            s = dot_nt(qi, kn)
+            seen = lax.broadcasted_iota(jnp.int32, (blk, blk), 0) >= lax.broadcasted_iota(jnp.int32, (blk, blk), 1)
+            diag = jnp.where(seen, s[:, lo:], -1e30)
+            s = jnp.concatenate([s[:, :lo], diag], axis=1) if lo else diag
+            e = jnp.exp((s - jnp.max(s, axis=1, keepdims=True)) * scale)
+            p = e * (1.0 / jnp.sum(e, axis=1, keepdims=True))
+            pb = p.astype(BF16)
+            ctxt[pl.ds(al(h, hd), hd), rows] = dot_nn(pb, vn).astype(BF16).T
+            dp_ = dot_nt(dci, vn).astype(BF16).astype(F32)
+            dsb = (p * (dp_ - jnp.sum(p * dp_, axis=1, keepdims=True)) * scale).astype(BF16)
+            dproj_v[rows, cols(0)] = unrope(dot_nn(dsb, kn), rows)
+            dk_s[:n, :] = dk_s[:n, :] + dot_tt(dsb, qi)
+            dv_s[:n, :] = dv_s[:n, :] + dot_tt(pb, dci)
+        if side == 1:
             @pl.loop(0, 4)
             def _(m):
                 at = pl.ds(al(m, blk), blk)
                 dproj_v[at, cols(1)] = unrope(dk_s[at, :], at)
                 dproj_v[at, cols(2)] = dv_s[at, :].astype(BF16)
+
+    def down(k):
+        ks = lax.rem(k, 2)
+        wait(load_d(k, ks))
+
+        @pl.when(k < 7)
+        def _():
+            start(load_d(k + 1, 1 - ks))
+
+        d_gelu = dot_nt(dy_v[...], wu_t[ks]).astype(BF16).astype(F32)
+        dh_v[:, pl.ds(al(k, 256), 256)] = (d_gelu * sl_buf[ks]).astype(BF16)
 
     def inputs(u):
         us = lax.rem(u, 2)
@@ -635,25 +645,25 @@
     def c_final(u):
         drain(cf1.at[u], cr_f1.at[u])
         for half in range(2):
-            c_loc[128 * half:128 * half + 128, pl.ds(al(u, 256), 256)] = c_blk(u, tp, half)[...].astype(F32) + (
+            sl_buf[u // 4, pl.ds(pl.multiple_of(lax.rem(u, 4) * 256 + 128 * half, 128), 128), :] = c_blk(u, tp, half)[...].astype(F32) + (
                 cf1[u, 0, half].astype(F32) + cf1[u, 1, half].astype(F32))
         drain(cl1.at[u], cs_l1.at[u])
         drain(cf1.at[u], cs_f1.at[u])
 
     def last():
-        wait(load_last())
+        drain(x_t, g_sem)
 
         @pl.loop(0, 8)
         def _(r):
-            at = pl.ds(al(r, 32), 32)
-            dy_at = pl.ds(pl.multiple_of(256 + r * 32, 32), 32)
+            def across(ref):
+                return jnp.concatenate([ref[u // 4, pl.ds(pl.multiple_of(256 * (u % 4) + r * 32, 32), 32), :] for u in range(8)], axis=1).astype(F32)
+
             own = pl.ds(pl.multiple_of(tp * 256 + r * 32, 32), 32)
-            mean, rstd = mean_ref[own, :], rstd_ref[own, :]
-            c = c_loc[at, :]
-            x_hat = (jnp.concatenate([a_buf[0, 0, at, :], a_buf[0, 1, at, :]], axis=1).astype(F32) - mean) * rstd
-            dy_own = jnp.concatenate([a_buf[0, 0, dy_at, :], a_buf[0, 1, dy_at, :]], axis=1).astype(F32)
+            rstd = rstd_ref[own, :]
+            c = across(sl_buf)
+            x_hat = (across(x_t) - mean_ref[own, :]) * rstd
             dx = rstd * (c - jnp.mean(c, axis=-1, keepdims=True) - x_hat * jnp.mean(c * x_hat, axis=-1, keepdims=True))
-            o_gx[at, :] = (dy_own + dx).astype(BF16)
+            o_gx[pl.ds(al(r, 32), 32), :] = (dy_v[own, :].astype(F32) + dx).astype(BF16)
 
     @pl.loop(0, STEPS)
     def _(p):
@@ -674,10 +684,28 @@
         def _():
             c_second(p - 18)
 
-        for i in range(4):
-            @pl.when((p < 16) & (lax.rem(p, 4) == i))
+        @pl.when(p < LATE)
+        def _():
+            slice_on(p)
+
+        @pl.when(p < LATE - 2)
+        def _():
+            slice_own(p + 2)
+
+        @pl.when((p >= 6) & (p < 14))
+        def _():
+            down(p - 6)
+
+        for side in range(2):
+            @pl.when((p >= 8) & (p < 16) & (lax.rem(p, 2) == side))
             def _():
-                attend(p // 4, i)
+                attend((p - 8) // 2, side)
+
+        @pl.when(p == 10)
+        def _():
+            for j in range(LATE):
+                for i in range(6):
+                    slice_copy(j, i).wait_send()
 
         @pl.when(p == 14)
         def _():
@@ -689,6 +717,7 @@
 
         @pl.when(p == 24)
         def _():
+            start(load_x())
             ln_send(0)
 
         for stage, me in ((1, tp), (2, y), (3, z)):
@@ -709,7 +738,7 @@
         drain(p_buf.at[p % 2, :, :, :, 0], ds.at[p % SLOTS])
 
 
-def back_call(get, hmt, hat, dy_full, d_hidden, qkv, d_ctx, w2, w_up, x_full, x_loc, dy_loc, ln_params, mean, rstd, cos_f, sin_f):
+def back_call(get, hmt, hat, dy_early, slope, qkv, w_out, w_down, w2, w_up, x_full, x_loc, dy_loc, ln_params, mean, rstd, cos_f, sin_f):
     hbm = pl.BlockSpec(memory_space=pl.ANY)
     vmem = pl.BlockSpec(memory_space=pltpu.VMEM)
     dma = pltpu.SemaphoreType.DMA
@@ -717,23 +746,23 @@
     k = (SLOTS,)
     return pl.pallas_call(
         back_kernel,
-        in_specs=[hbm] * 12 + [vmem] * 5,
+        in_specs=[hbm] * 13 + [vmem] * 5,
         out_specs=[vmem] * 6,
         out_shape=[shape((256, 2048), BF16), shape((4, 2048), F32), shape((64, 1536), F32), shape((16, 2048), F32),
                    shape((64, 2048), F32), shape((64, 2048), F32)],
         scratch_shapes=[
-            pltpu.VMEM((2, 2, 1024, 1024), BF16), pltpu.VMEM((2, 1024, 256), BF16),
+            pltpu.VMEM((2, 1024, 1024), BF16), pltpu.VMEM((2, 1024, 256), BF16),
             pltpu.VMEM((2, 2, 4, 4, 2, 64, 128), F32), pltpu.VMEM(k + (2, 4, 4, 64, 128), F32),
             pltpu.VMEM(k + (2, 2, 4, 32, 128), F32), pltpu.VMEM(k + (2, 2, 2, 4, 32, 128), F32),
             pltpu.VMEM(k + (2, 2, 32, 128), F32), pltpu.VMEM(k + (2, 2, 2, 32, 128), F32),
             pltpu.VMEM((4, 4, 4, 2048), F32),
             pltpu.VMEM((1024, 2048), BF16), pltpu.VMEM((1024, 1536), BF16), pltpu.VMEM((512, 1024), BF16),
-            pltpu.VMEM((2, 1024, 384), BF16), pltpu.VMEM((2, 1024, 128), BF16),
+            pltpu.VMEM((2, 1024, 384), BF16), pltpu.VMEM((1024, 128), BF16),
             pltpu.VMEM((1024, 128), F32), pltpu.VMEM((1024, 128), F32),
             pltpu.VMEM((2, 256, 1536), BF16), pltpu.VMEM((2, 256, 2048), BF16), pltpu.VMEM((2, 1024, 256), BF16),
             pltpu.VMEM((5, 4, 256, 256), BF16), pltpu.VMEM((8, 2, 128, 256), BF16), pltpu.VMEM((8, 2, 2, 128, 256), BF16),
-            pltpu.VMEM((256, 2048), F32),
-            dma((2, 2)), dma((2,)), dma, dma((2, 2)), dma((2, 3)), dma((2, 2)),
+            pltpu.VMEM((2, 1024, 256), F32), pltpu.VMEM((1024, 2048), BF16), pltpu.VMEM((2, 128, 2048), BF16),
+            dma((2,)), dma((2,)), dma((2, 2)), dma((2, 3)), dma((2, 2)), dma, dma((LATE, 6)), dma((LATE, 6)),
             dma(k), dma(k), dma(k), dma(k), dma(k), dma(k), dma(k), dma(k), dma(k), dma(k),
             dma((4,)), dma((4,)), dma((8,)), dma((8,)), dma((8,)), dma((8,)),
             pltpu.SemaphoreType.REGULAR((5,)),
@@ -741,7 +770,7 @@
         compiler_params=pltpu.CompilerParams(collective_id=0, has_side_effects=True, vmem_limit_bytes=65400 * 1024),
         cost_estimate=pl.CostEstimate(flops=50_000_000_000, bytes_accessed=100_000_000, transcendentals=0),
         name='back',
-    )(get, hmt, hat, dy_full, d_hidden, qkv, d_ctx, w2, w_up, x_full, x_loc, dy_loc, ln_params, mean, rstd, cos_f, sin_f)
+    )(get, hmt, hat, dy_early, slope, qkv, w_out, w_down, w2, w_up, x_full, x_loc, dy_loc, ln_params, mean, rstd, cos_f, sin_f)
 
 
 def solution(mesh):
@@ -749,10 +778,9 @@
         width, groups, slots, head_dim = w_qkv.shape
         cos_f, sin_f = (jnp.asarray(t) for t in rope_tables(4 * x_loc.shape[1], head_dim))
         w_rows = w_qkv.transpose(0, 2, 1, 3).reshape(width * slots * groups, head_dim)
-        x_full, dy_full, hat, hmt, qkv, get, d_hidden, d_ctx, w2, mean, rstd = front_call(
-            x_loc[0], dy_loc[0], ln_params, cos_f, sin_f, w_rows, w_up, w_down, w_out)
+        x_full, dy_early, hat, hmt, qkv, get, slope, w2, mean, rstd = front_call(x_loc[0], dy_loc[0], ln_params, cos_f, sin_f, w_rows, w_up)
         grad_x, g_ln, g_qkv, g_out, g_up, g_down = back_call(
-            get, hmt, hat, dy_full, d_hidden, qkv, d_ctx, w2, w_up, x_full, x_loc[0], dy_loc[0], ln_params, mean, rstd, cos_f, sin_f)
+            get, hmt, hat, dy_early, slope, qkv, w_out, w_down, w2, w_up, x_full, x_loc[0], dy_loc[0], ln_params, mean, rstd, cos_f, sin_f)
         return grad_x[None], g_ln, g_qkv.reshape(64, groups, slots, head_dim), g_out, g_up, g_down
 
     act_spec = P('dp', 'tp', None)

time: 243 us -> 238 us (0.979)
  Pallas kernels: 233 us -> 228 us
    pallas_call x1, Pallas kernels: 79.3 us -> 58.3 us  [front_call(): pl.pallas_call(front_kernel, in_specs=[hbm, hbm, vmem, vmem, vmem, hbm, h...]
    pallas_call x1, Pallas kernels: 154 us -> 170 us  [back_call(): pl.pallas_call(back_kernel, in_specs=[hbm] * 13 + [vmem] * 5, out_specs=[...]
where the time goes in v2:
time: 238 us
  Pallas kernels  228 us (96%)
  local copies, waits for them, and re-layouts  9.05 us (4%)
    pallas_call x1, Pallas kernels, back_call(): pl.pallas_call(back_kernel, in_specs=[hbm] * 13 + [vmem] * 5, out_specs=[...  170 us
    pallas_call x1, Pallas kernels, front_call(): pl.pallas_call(front_kernel, in_specs=[hbm, hbm, vmem, vmem, vmem, hbm, h...  58.3 us
    unnamed x10, local copies, waits for them, and re-layouts  7.69 us

profile of v2, /device:TPU:0, one launch (start us, length us, event | category | flops | bytes accessed | tf_op | source)
XLA Modules:
  0.0 237.8 jit_solution(1203892274456131103)
XLA Ops:
  0.6 58.3 %front.1 = (bf16[1024,2048]{1,0:T(8,128)(2,1)}, bf16[1024,768]{1,0:T(8,128)(2,1)}, bf16[2048,1024]{1,0:T(8,128)(2,1)}, bf16[2048,1024]{1,0:T(8,128)(2,1)}, bf16[...) custom-call(bf16[256,2048]{1,0:T(8,128)(2,1)} %bitcast.8, ...), custom_call_target="tpu_custom_call" | custom-call | flops 15032385536 | bytes 70000000 | tf_op jit(solution)/shard_map/front/pallas_call | solution.py:231
  58.9 169.9 %back.1 = (bf16[256,2048]{1,0:T(8,128)(2,1)}, f32[4,2048]{1,0:T(4,128)}, f32[64,1536]{1,0:T(8,128)}, f32[16,2048]{1,0:T(8,128)}, f32[64,2048]{1,0:T(8,128)}, /*index=5*/f32[64,2048]{1,0:T(8,128)}) custom-call(bf16[2048,1024]{1,0:T(8,128)(2,1)} %get-tuple-element.22.get_ref, bf16[2048,1024]{1,0:T(8,128)(2,1)} %get-tuple-element.23.hmt_ref, ...), custom_call_target="tpu_custom_call" | custom-call | flops 49999998976 | bytes 100000000 | tf_op jit(solution)/shard_map/back/pallas_call | solution.py:747
  228.8 0.0 copy-start.1
  228.8 0.0 copy-start
  228.8 1.4 reshape.19
  230.1 0.8 copy.16
  231.0 2.3 copy.22
  233.3 1.4 copy.23
  234.7 1.6 copy.24
  236.2 0.0 copy-done.1
  236.2 0.8 copy.25
  237.0 0.0 copy-done
  237.0 0.8 copy.26
Async XLA Ops:
  228.8 7.5 %copy-start.1 = (f32[64,2048]{1,0:T(8,128)S(1)}, f32[64,2048]{1,0:T(8,128)}, u32[]{:S(2)}) copy-start(f32[64,2048]{1,0:T(8,128)} %get-tuple-element.60) | copy-start | bytes 1572868
  228.8 8.3 %copy-start = (f32[64,2048]{1,0:T(8,128)S(1)}, f32[64,2048]{1,0:T(8,128)}, u32[]{:S(2)}) copy-start(f32[64,2048]{1,0:T(8,128)} %get-tuple-element.61) | copy-start | bytes 1572868

commit v3 on v2

--- a/solution.py
+++ b/solution.py
@@ -12,10 +12,11 @@
 ROPE_BASE = 10000.0
 MESH = pl.DeviceIdType.MESH
 PIECES = 24
-SLOTS = 8
-STEPS = PIECES + 7
+SLOTS = 10
+STEPS = PIECES + 9
 EARLY = 768
 LATE = 5
+VMEM_LIMIT = 60000 * 1024
 F32 = jnp.float32
 BF16 = jnp.bfloat16
 
@@ -671,18 +672,18 @@
         def _():
             compute(p)
 
-        for lag, stage in ((7, stage_f2), (6, stage_l2), (5, stage_f1), (3, stage_l1), (1, stage_s)):
+        for lag, stage in ((9, stage_f2), (8, stage_l2), (7, stage_f1), (4, stage_l1), (1, stage_s)):
             @pl.when((p >= lag) & (p < PIECES + lag))
             def _():
                 stage(p - lag)
 
+        @pl.when((p >= 22) & (p < 30))
+        def _():
+            c_final(p - 22)
+
         @pl.when((p >= 20) & (p < 28))
         def _():
-            c_final(p - 20)
-
-        @pl.when((p >= 18) & (p < 26))
-        def _():
-            c_second(p - 18)
+            c_second(p - 20)
 
         @pl.when(p < LATE)
         def _():
@@ -696,10 +697,10 @@
         def _():
             down(p - 6)
 
-        for side in range(2):
-            @pl.when((p >= 8) & (p < 16) & (lax.rem(p, 2) == side))
+        for side, steps in enumerate(((7, 11, 14, 16), (9, 13, 15, 17))):
+            @pl.when((p == steps[0]) | (p == steps[1]) | (p == steps[2]) | (p == steps[3]))
             def _():
-                attend((p - 8) // 2, side)
+                attend(sum((p >= at).astype(jnp.int32) for at in steps[1:]), side)
 
         @pl.when(p == 10)
         def _():
@@ -711,26 +712,26 @@
         def _():
             start(load_t(0, 0))
 
-        @pl.when((p >= 16) & (p < 24))
-        def _():
-            inputs(p - 16)
-
-        @pl.when(p == 24)
+        @pl.when((p >= 18) & (p < 26))
+        def _():
+            inputs(p - 18)
+
+        @pl.when(p == 26)
         def _():
             start(load_x())
             ln_send(0)
 
         for stage, me in ((1, tp), (2, y), (3, z)):
-            @pl.when(p == 24 + stage)
+            @pl.when(p == 26 + stage)
             def _():
                 lnb[stage, me] = ln_sum(stage - 1)
                 ln_send(stage)
 
-        @pl.when(p == 28)
+        @pl.when(p == 30)
         def _():
             last()
 
-        @pl.when(p == 29)
+        @pl.when(p == 30)
         def _():
             o_ln[...] = ln_sum(3)
 
@@ -773,6 +774,42 @@
     )(get, hmt, hat, dy_early, slope, qkv, w_out, w_down, w2, w_up, x_full, x_loc, dy_loc, ln_params, mean, rstd, cos_f, sin_f)
 
 
+def place_kernel(gx, ln, qkv, out, up, down, o_gx, o_ln, o_qkv, o_out, o_up, o_down, b_gx, b_ln, b_qkv, b_out, b_up, b_down, b_rows, in_sem, out_sem):
+    ins = [pltpu.make_async_copy(src, buf, in_sem.at[i]) for i, (src, buf) in enumerate(
+        ((qkv, b_qkv), (gx, b_gx), (ln, b_ln), (out, b_out), (up, b_up), (down, b_down)))]
+    outs = [pltpu.make_async_copy(buf, dst, out_sem.at[i]) for i, (buf, dst) in enumerate(
+        ((b_rows, o_qkv), (b_gx, o_gx), (b_ln, o_ln), (b_out, o_out), (b_up, o_up), (b_down, o_down)))]
+    for copy in ins:
+        copy.start()
+    for i in range(1, 6):
+        ins[i].wait()
+        outs[i].start()
+    ins[0].wait()
+    for g in range(4):
+        for j in range(3):
+            b_rows[:, j, g, :] = b_qkv[:, g * 384 + j * 128:g * 384 + j * 128 + 128]
+    outs[0].start()
+    for copy in outs:
+        copy.wait()
+
+
+def place_call(gx, ln, qkv, out, up, down):
+    hbm = pl.BlockSpec(memory_space=pl.ANY)
+    dma = pltpu.SemaphoreType.DMA
+    arrays = (gx, ln, qkv, out, up, down)
+    rows = (qkv.shape[0], 3, 4, 128)
+    shapes = [jax.ShapeDtypeStruct(rows if v is qkv else v.shape, v.dtype) for v in arrays]
+    return pl.pallas_call(
+        place_kernel,
+        in_specs=[hbm] * 6,
+        out_specs=[hbm] * 6,
+        out_shape=shapes,
+        scratch_shapes=[pltpu.VMEM(v.shape, v.dtype) for v in arrays] + [pltpu.VMEM(rows, F32), dma((6,)), dma((6,))],
+        compiler_params=pltpu.CompilerParams(vmem_limit_bytes=VMEM_LIMIT),
+        name='place',
+    )(*arrays)
+
+
 def solution(mesh):
     def local_step(x_loc, dy_loc, ln_params, w_qkv, w_out, w_up, w_down):
         width, groups, slots, head_dim = w_qkv.shape
@@ -781,7 +818,8 @@
         x_full, dy_early, hat, hmt, qkv, get, slope, w2, mean, rstd = front_call(x_loc[0], dy_loc[0], ln_params, cos_f, sin_f, w_rows, w_up)
         grad_x, g_ln, g_qkv, g_out, g_up, g_down = back_call(
             get, hmt, hat, dy_early, slope, qkv, w_out, w_down, w2, w_up, x_full, x_loc[0], dy_loc[0], ln_params, mean, rstd, cos_f, sin_f)
-        return grad_x[None], g_ln, g_qkv.reshape(64, groups, slots, head_dim), g_out, g_up, g_down
+        grad_x, g_ln, g_qkv, g_out, g_up, g_down = place_call(grad_x, g_ln, g_qkv, g_out, g_up, g_down)
+        return grad_x[None], g_ln, g_qkv.transpose(0, 2, 1, 3), g_out, g_up, g_down
 
     act_spec = P('dp', 'tp', None)
     in_specs = (act_spec, act_spec, P(None, None), P(None, 'tp', None, None), P('tp', None), P(None, 'tp'), P('tp', None))

time: 238 us -> 232 us (0.975)
  local copies, waits for them, and re-layouts: 9.05 us -> 0 us
  Pallas kernels: 228 us -> 231 us
    unnamed x10 -> x0, local copies, waits for them, and re-layouts: 7.69 us -> none
    pallas_call x0 -> x1, Pallas kernels: none -> 2.95 us  [place_call(): pl.pallas_call(place_kernel, in_specs=[hbm] * 6, out_specs=[hbm] * 6, out...]
where the time goes in v3:
time: 232 us; the launch traced here: 231 us
  Pallas kernels  231 us (100%)
    pallas_call x1, Pallas kernels, back_call(): pl.pallas_call(back_kernel, in_specs=[hbm] * 13 + [vmem] * 5, out_specs=[...  169 us
    pallas_call x1, Pallas kernels, front_call(): pl.pallas_call(front_kernel, in_specs=[hbm, hbm, vmem, vmem, vmem, hbm, h...  58.2 us

profile of v3, /device:TPU:0, one launch (start us, length us, event | category | flops | bytes accessed | tf_op | source)
XLA Modules:
  0.0 231.4 jit_solution(1054628206152785606)
XLA Ops:
  0.6 58.2 %front.1 = (bf16[1024,2048]{1,0:T(8,128)(2,1)}, bf16[1024,768]{1,0:T(8,128)(2,1)}, bf16[2048,1024]{1,0:T(8,128)(2,1)}, bf16[2048,1024]{1,0:T(8,128)(2,1)}, bf16[...) custom-call(bf16[256,2048]{1,0:T(8,128)(2,1)} %bitcast.8, ...), custom_call_target="tpu_custom_call" | custom-call | flops 15032385536 | bytes 70000000 | tf_op jit(solution)/shard_map/front/pallas_call | solution.py:232
  58.9 169.4 %back.1 = (bf16[256,2048]{1,0:T(8,128)(2,1)}, f32[4,2048]{1,0:T(4,128)}, f32[64,1536]{1,0:T(8,128)}, f32[16,2048]{1,0:T(8,128)}, f32[64,2048]{1,0:T(8,128)}, /*index=5*/f32[64,2048]{1,0:T(8,128)}) custom-call(bf16[2048,1024]{1,0:T(8,128)(2,1)} %get-tuple-element.28.get_ref, bf16[2048,1024]{1,0:T(8,128)(2,1)} %get-tuple-element.29.hmt_ref, ...), custom_call_target="tpu_custom_call" | custom-call | flops 49999998976 | bytes 100000000 | tf_op jit(solution)/shard_map/back/pallas_call | solution.py:748
  228.3 3.0 %place.1 = (bf16[256,2048]{1,0:T(8,128)(2,1)}, f32[4,2048]{1,0:T(4,128)}, f32[64,3,4,128]{3,2,1,0:T(4,128)}, f32[16,2048]{1,0:T(8,128)}, f32[64,2048]{1,0:T(8,128)}, /*index=5*/f32[64,2048]{1,0:T(8,128)}) custom-call(bf16[256,2048]{1,0:T(8,128)(2,1)} %get-tuple-element.38.gx, f32[4,2048]{1,0:T(4,128)} %get-tuple-element.39.ln, ...), custom_call_target="tpu_custom_call" | custom-call | tf_op jit(solution)/shard_map/place/pallas_call | solution.py:802

commit v4 on v3

--- a/solution.py
+++ b/solution.py
@@ -12,8 +12,8 @@
 ROPE_BASE = 10000.0
 MESH = pl.DeviceIdType.MESH
 PIECES = 24
-SLOTS = 10
-STEPS = PIECES + 9
+SLOTS = 8
+STEPS = PIECES + 7
 EARLY = 768
 LATE = 5
 VMEM_LIMIT = 60000 * 1024
@@ -256,7 +256,7 @@
                 ln_ref, mean_ref, rstd_ref, cos_ref, sin_ref,
                 o_gx, o_ln, o_qkv, o_out, o_up, o_down,
                 a_buf, b_buf, p_buf, d_buf, l1, f1, l2, f2, lnb, dh_v, dproj_v, ctxt, qkv_b, dctx_b, dk_s, dv_s,
-                wq_t, wu_t, x_t, c_buf, cl1, cf1, sl_buf, dy_v, wo_t,
+                wq_t, wu_t, x_t, c_buf, cl1, cf1, sl_buf, dy_v, wo_t, kt, vt,
                 a_sem, dy_sem, h_sem, t_sem, d_sem, g_sem, gs, gr, ds, dr, s_l1, r_l1, s_f1, r_f1, s_l2, r_l2, s_f2, r_f2, ln_s, ln_r,
                 cs_l1, cr_l1, cs_f1, cr_f1, credit):
     tp = lax.axis_index('tp')
@@ -478,10 +478,10 @@
         ps = lax.rem(q, 2)
         drain(d_buf.at[slot], dr.at[slot])
 
-        @pl.loop(0, 32)
+        @pl.loop(0, 8)
         def _(i):
-            col, zi, yi = i // 16, lax.rem(i // 4, 4), lax.rem(i, 4)
-            d_buf[slot, col, zi, yi] = d_buf[slot, col, zi, yi] + p_buf[ps, col, zi, yi, core]
+            col, zi = i // 4, lax.rem(i, 4)
+            d_buf[slot, col, zi] = d_buf[slot, col, zi] + p_buf[ps, col, zi, :, core]
 
         @pl.when(q >= SLOTS)
         def _():
@@ -566,6 +566,8 @@
                 start(load_head(h + 1, 1 - hs))
 
             dctx_b[...] = dot_nt(dy_v[...], wo_t[hs]).astype(BF16)
+            kt[...] = qkv_b[hs, :, hd:2 * hd].T
+            vt[...] = qkv_b[hs, :, 2 * hd:3 * hd].T
             dk_s[...] = jnp.zeros_like(dk_s)
             dv_s[...] = jnp.zeros_like(dv_s)
 
@@ -573,19 +575,19 @@
             rows, lo, n = slice(i * blk, (i + 1) * blk), i * blk, (i + 1) * blk
             qi, dci = qkv_b[hs, rows, 0:hd], dctx_b[rows, :]
             kn, vn = qkv_b[hs, :n, hd:2 * hd], qkv_b[hs, :n, 2 * hd:3 * hd]
-            s = dot_nt(qi, kn)
-            seen = lax.broadcasted_iota(jnp.int32, (blk, blk), 0) >= lax.broadcasted_iota(jnp.int32, (blk, blk), 1)
-            diag = jnp.where(seen, s[:, lo:], -1e30)
-            s = jnp.concatenate([s[:, :lo], diag], axis=1) if lo else diag
-            e = jnp.exp((s - jnp.max(s, axis=1, keepdims=True)) * scale)
-            p = e * (1.0 / jnp.sum(e, axis=1, keepdims=True))
+            s = dot_nt(kn, qi)
+            seen = lax.broadcasted_iota(jnp.int32, (blk, blk), 0) <= lax.broadcasted_iota(jnp.int32, (blk, blk), 1)
+            diag = jnp.where(seen, s[lo:, :], -1e30)
+            s = jnp.concatenate([s[:lo, :], diag], axis=0) if lo else diag
+            e = jnp.exp((s - jnp.max(s, axis=0, keepdims=True)) * scale)
+            p = e * (1.0 / jnp.sum(e, axis=0, keepdims=True))
             pb = p.astype(BF16)
-            ctxt[pl.ds(al(h, hd), hd), rows] = dot_nn(pb, vn).astype(BF16).T
-            dp_ = dot_nt(dci, vn).astype(BF16).astype(F32)
-            dsb = (p * (dp_ - jnp.sum(p * dp_, axis=1, keepdims=True)) * scale).astype(BF16)
-            dproj_v[rows, cols(0)] = unrope(dot_nn(dsb, kn), rows)
-            dk_s[:n, :] = dk_s[:n, :] + dot_tt(dsb, qi)
-            dv_s[:n, :] = dv_s[:n, :] + dot_tt(pb, dci)
+            ctxt[pl.ds(al(h, hd), hd), rows] = dot_nn(vt[:, :n], pb).astype(BF16)
+            dp_ = dot_nt(vn, dci).astype(BF16).astype(F32)
+            dsb = (p * (dp_ - jnp.sum(p * dp_, axis=0, keepdims=True)) * scale).astype(BF16)
+            dproj_v[rows, cols(0)] = unrope(dot_nn(kt[:, :n], dsb).T, rows)
+            dk_s[:n, :] = dk_s[:n, :] + dot_nn(dsb, qi)
+            dv_s[:n, :] = dv_s[:n, :] + dot_nn(pb, dci)
         if side == 1:
             @pl.loop(0, 4)
             def _(m):
@@ -672,7 +674,7 @@
         def _():
             compute(p)
 
-        for lag, stage in ((9, stage_f2), (8, stage_l2), (7, stage_f1), (4, stage_l1), (1, stage_s)):
+        for lag, stage in ((7, stage_f2), (6, stage_l2), (5, stage_f1), (3, stage_l1), (1, stage_s)):
             @pl.when((p >= lag) & (p < PIECES + lag))
             def _():
                 stage(p - lag)
@@ -763,6 +765,7 @@
             pltpu.VMEM((2, 256, 1536), BF16), pltpu.VMEM((2, 256, 2048), BF16), pltpu.VMEM((2, 1024, 256), BF16),
             pltpu.VMEM((5, 4, 256, 256), BF16), pltpu.VMEM((8, 2, 128, 256), BF16), pltpu.VMEM((8, 2, 2, 128, 256), BF16),
             pltpu.VMEM((2, 1024, 256), F32), pltpu.VMEM((1024, 2048), BF16), pltpu.VMEM((2, 128, 2048), BF16),
+            pltpu.VMEM((128, 1024), BF16), pltpu.VMEM((128, 1024), BF16),
             dma((2,)), dma((2,)), dma((2, 2)), dma((2, 3)), dma((2, 2)), dma, dma((LATE, 6)), dma((LATE, 6)),
             dma(k), dma(k), dma(k), dma(k), dma(k), dma(k), dma(k), dma(k), dma(k), dma(k),
             dma((4,)), dma((4,)), dma((8,)), dma((8,)), dma((8,)), dma((8,)),

time: 232 us -> 224 us (0.966)
  Pallas kernels: 231 us -> 223 us
    pallas_call x1, Pallas kernels: 169 us -> 161 us  [back_call(): pl.pallas_call(back_kernel, in_specs=[hbm] * 13 + [vmem] * 5, out_specs=[...]
where the time goes in v4:
time: 224 us; the launch traced here: 223 us
  Pallas kernels  223 us (100%)
    pallas_call x1, Pallas kernels, back_call(): pl.pallas_call(back_kernel, in_specs=[hbm] * 13 + [vmem] * 5, out_specs=[...  161 us
    pallas_call x1, Pallas kernels, front_call(): pl.pallas_call(front_kernel, in_specs=[hbm, hbm, vmem, vmem, vmem, hbm, h...  58.2 us

profile of v4, /device:TPU:0, one launch (start us, length us, event | category | flops | bytes accessed | tf_op | source)
XLA Modules:
  0.0 223.4 jit_solution(17788019839883858454)
XLA Ops:
  0.6 58.2 %front.1 = (bf16[1024,2048]{1,0:T(8,128)(2,1)}, bf16[1024,768]{1,0:T(8,128)(2,1)}, bf16[2048,1024]{1,0:T(8,128)(2,1)}, bf16[2048,1024]{1,0:T(8,128)(2,1)}, bf16[...) custom-call(bf16[256,2048]{1,0:T(8,128)(2,1)} %bitcast.8, ...), custom_call_target="tpu_custom_call" | custom-call | flops 15032385536 | bytes 70000000 | tf_op jit(solution)/shard_map/front/pallas_call | solution.py:232
  58.9 161.4 %back.1 = (bf16[256,2048]{1,0:T(8,128)(2,1)}, f32[4,2048]{1,0:T(4,128)}, f32[64,1536]{1,0:T(8,128)}, f32[16,2048]{1,0:T(8,128)}, f32[64,2048]{1,0:T(8,128)}, /*index=5*/f32[64,2048]{1,0:T(8,128)}) custom-call(bf16[2048,1024]{1,0:T(8,128)(2,1)} %get-tuple-element.28.get_ref, bf16[2048,1024]{1,0:T(8,128)(2,1)} %get-tuple-element.29.hmt_ref, ...), custom_call_target="tpu_custom_call" | custom-call | flops 49999998976 | bytes 100000000 | tf_op jit(solution)/shard_map/back/pallas_call | solution.py:750
  220.3 3.0 %place.1 = (bf16[256,2048]{1,0:T(8,128)(2,1)}, f32[4,2048]{1,0:T(4,128)}, f32[64,3,4,128]{3,2,1,0:T(4,128)}, f32[16,2048]{1,0:T(8,128)}, f32[64,2048]{1,0:T(8,128)}, /*index=5*/f32[64,2048]{1,0:T(8,128)}) custom-call(bf16[256,2048]{1,0:T(8,128)(2,1)} %get-tuple-element.38.gx, f32[4,2048]{1,0:T(4,128)} %get-tuple-element.39.ln, ...), custom_call_target="tpu_custom_call" | custom-call | tf_op jit(solution)/shard_map/place/pallas_call | solution.py:805

commit v5 on v4

--- a/solution.py
+++ b/solution.py
@@ -14,8 +14,8 @@
 PIECES = 24
 SLOTS = 8
 STEPS = PIECES + 7
-EARLY = 768
-LATE = 5
+EARLY = 512
+LATE = 6
 VMEM_LIMIT = 60000 * 1024
 F32 = jnp.float32
 BF16 = jnp.bfloat16
@@ -394,15 +394,11 @@
         def _():
             early.wait()
 
-        @pl.when(p == 3)
+        @pl.when(p == 2)
         def _():
             late.wait()
 
-        @pl.when((p >= 3) & (p < 7))
-        def _():
-            slice_done(p - 3)
-
-        @pl.when(p == 6)
+        @pl.when((p >= 2) & (p < 8))
         def _():
             slice_done(p - 2)
 
@@ -695,9 +691,9 @@
         def _():
             slice_own(p + 2)
 
-        @pl.when((p >= 6) & (p < 14))
-        def _():
-            down(p - 6)
+        @pl.when((p >= 7) & (p < 15))
+        def _():
+            down(p - 7)
 
         for side, steps in enumerate(((7, 11, 14, 16), (9, 13, 15, 17))):
             @pl.when((p == steps[0]) | (p == steps[1]) | (p == steps[2]) | (p == steps[3]))

time: 224 us -> 226 us (level)
    pallas_call x1, Pallas kernels: 161 us -> 165 us  [back_call(): pl.pallas_call(back_kernel, in_specs=[hbm] * 13 + [vmem] * 5, out_specs=[...]
where the time goes in v5:
time: 226 us
  Pallas kernels  225 us (100%)
    pallas_call x1, Pallas kernels, back_call(): pl.pallas_call(back_kernel, in_specs=[hbm] * 13 + [vmem] * 5, out_specs=[...  165 us
    pallas_call x1, Pallas kernels, front_call(): pl.pallas_call(front_kernel, in_specs=[hbm, hbm, vmem, vmem, vmem, hbm, h...  56.8 us

profile of v5, /device:TPU:0, one launch (start us, length us, event | category | flops | bytes accessed | tf_op | source)
XLA Modules:
  0.0 225.9 jit_solution(1971158812094101043)
XLA Ops:
  0.6 56.8 %front.1 = (bf16[1024,2048]{1,0:T(8,128)(2,1)}, bf16[1024,512]{1,0:T(8,128)(2,1)}, bf16[2048,1024]{1,0:T(8,128)(2,1)}, bf16[2048,1024]{1,0:T(8,128)(2,1)}, bf16[...) custom-call(bf16[256,2048]{1,0:T(8,128)(2,1)} %bitcast.8, ...), custom_call_target="tpu_custom_call" | custom-call | flops 15032385536 | bytes 70000000 | tf_op jit(solution)/shard_map/front/pallas_call | solution.py:232
  57.4 165.4 %back.1 = (bf16[256,2048]{1,0:T(8,128)(2,1)}, f32[4,2048]{1,0:T(4,128)}, f32[64,1536]{1,0:T(8,128)}, f32[16,2048]{1,0:T(8,128)}, f32[64,2048]{1,0:T(8,128)}, /*index=5*/f32[64,2048]{1,0:T(8,128)}) custom-call(bf16[2048,1024]{1,0:T(8,128)(2,1)} %get-tuple-element.28.get_ref, bf16[2048,1024]{1,0:T(8,128)(2,1)} %get-tuple-element.29.hmt_ref, ...), custom_call_target="tpu_custom_call" | custom-call | flops 49999998976 | bytes 100000000 | tf_op jit(solution)/shard_map/back/pallas_call | solution.py:746
  222.8 3.0 %place.1 = (bf16[256,2048]{1,0:T(8,128)(2,1)}, f32[4,2048]{1,0:T(4,128)}, f32[64,3,4,128]{3,2,1,0:T(4,128)}, f32[16,2048]{1,0:T(8,128)}, f32[64,2048]{1,0:T(8,128)}, /*index=5*/f32[64,2048]{1,0:T(8,128)}) custom-call(bf16[256,2048]{1,0:T(8,128)(2,1)} %get-tuple-element.38.gx, f32[4,2048]{1,0:T(4,128)} %get-tuple-element.39.ln, ...), custom_call_target="tpu_custom_call" | custom-call | tf_op jit(solution)/shard_map/place/pallas_call | solution.py:801

commit v6 on v4

--- a/solution.py
+++ b/solution.py
@@ -398,13 +398,14 @@
         def _():
             late.wait()
 
-        @pl.when((p >= 3) & (p < 7))
+        @pl.when((p >= 3) & (p < 6))
         def _():
             slice_done(p - 3)
 
-        @pl.when(p == 6)
+        @pl.when(p == 5)
         def _():
             slice_done(p - 2)
+            slice_done(p - 1)
 
         @pl.when(p < 8)
         def _():
@@ -674,32 +675,32 @@
         def _():
             compute(p)
 
+        @pl.when(p < LATE)
+        def _():
+            slice_on(p)
+
+        @pl.when(p < LATE - 2)
+        def _():
+            slice_own(p + 2)
+
         for lag, stage in ((7, stage_f2), (6, stage_l2), (5, stage_f1), (3, stage_l1), (1, stage_s)):
             @pl.when((p >= lag) & (p < PIECES + lag))
             def _():
                 stage(p - lag)
 
-        @pl.when((p >= 22) & (p < 30))
-        def _():
-            c_final(p - 22)
-
-        @pl.when((p >= 20) & (p < 28))
-        def _():
-            c_second(p - 20)
-
-        @pl.when(p < LATE)
-        def _():
-            slice_on(p)
-
-        @pl.when(p < LATE - 2)
-        def _():
-            slice_own(p + 2)
-
-        @pl.when((p >= 6) & (p < 14))
-        def _():
-            down(p - 6)
-
-        for side, steps in enumerate(((7, 11, 14, 16), (9, 13, 15, 17))):
+        @pl.when((p >= 21) & (p < 29))
+        def _():
+            c_final(p - 21)
+
+        @pl.when((p >= 19) & (p < 27))
+        def _():
+            c_second(p - 19)
+
+        @pl.when((p >= 5) & (p < 13))
+        def _():
+            down(p - 5)
+
+        for side, steps in enumerate(((6, 9, 12, 15), (7, 10, 13, 16))):
             @pl.when((p == steps[0]) | (p == steps[1]) | (p == steps[2]) | (p == steps[3]))
             def _():
                 attend(sum((p >= at).astype(jnp.int32) for at in steps[1:]), side)
@@ -714,26 +715,26 @@
         def _():
             start(load_t(0, 0))
 
-        @pl.when((p >= 18) & (p < 26))
-        def _():
-            inputs(p - 18)
-
-        @pl.when(p == 26)
+        @pl.when((p >= 17) & (p < 25))
+        def _():
+            inputs(p - 17)
+
+        @pl.when(p == 25)
         def _():
             start(load_x())
             ln_send(0)
 
         for stage, me in ((1, tp), (2, y), (3, z)):
-            @pl.when(p == 26 + stage)
+            @pl.when(p == 25 + stage)
             def _():
                 lnb[stage, me] = ln_sum(stage - 1)
                 ln_send(stage)
 
-        @pl.when(p == 30)
+        @pl.when(p == 29)
         def _():
             last()
 
-        @pl.when(p == 30)
+        @pl.when(p == 29)
         def _():
             o_ln[...] = ln_sum(3)
 

time: 224 us -> 226 us (level)
  no operation moved by 1% of the time
where the time goes in v6:
time: 226 us
  Pallas kernels  225 us (100%)
    pallas_call x1, Pallas kernels, back_call(): pl.pallas_call(back_kernel, in_specs=[hbm] * 13 + [vmem] * 5, out_specs=[...  164 us
    pallas_call x1, Pallas kernels, front_call(): pl.pallas_call(front_kernel, in_specs=[hbm, hbm, vmem, vmem, vmem, hbm, h...  58.2 us

profile of v6, /device:TPU:0, one launch (start us, length us, event | category | flops | bytes accessed | tf_op | source)
XLA Modules:
  0.0 225.5 jit_solution(1015145562497923259)
XLA Ops:
  0.6 58.2 %front.1 = (bf16[1024,2048]{1,0:T(8,128)(2,1)}, bf16[1024,768]{1,0:T(8,128)(2,1)}, bf16[2048,1024]{1,0:T(8,128)(2,1)}, bf16[2048,1024]{1,0:T(8,128)(2,1)}, bf16[...) custom-call(bf16[256,2048]{1,0:T(8,128)(2,1)} %bitcast.8, ...), custom_call_target="tpu_custom_call" | custom-call | flops 15032385536 | bytes 70000000 | tf_op jit(solution)/shard_map/front/pallas_call | solution.py:232
  58.9 163.5 %back.1 = (bf16[256,2048]{1,0:T(8,128)(2,1)}, f32[4,2048]{1,0:T(4,128)}, f32[64,1536]{1,0:T(8,128)}, f32[16,2048]{1,0:T(8,128)}, f32[64,2048]{1,0:T(8,128)}, /*index=5*/f32[64,2048]{1,0:T(8,128)}) custom-call(bf16[2048,1024]{1,0:T(8,128)(2,1)} %get-tuple-element.28.get_ref, bf16[2048,1024]{1,0:T(8,128)(2,1)} %get-tuple-element.29.hmt_ref, ...), custom_call_target="tpu_custom_call" | custom-call | flops 49999998976 | bytes 100000000 | tf_op jit(solution)/shard_map/back/pallas_call | solution.py:751
  222.4 3.0 %place.1 = (bf16[256,2048]{1,0:T(8,128)(2,1)}, f32[4,2048]{1,0:T(4,128)}, f32[64,3,4,128]{3,2,1,0:T(4,128)}, f32[16,2048]{1,0:T(8,128)}, f32[64,2048]{1,0:T(8,128)}, /*index=5*/f32[64,2048]{1,0:T(8,128)}) custom-call(bf16[256,2048]{1,0:T(8,128)(2,1)} %get-tuple-element.38.gx, f32[4,2048]{1,0:T(4,128)} %get-tuple-element.39.ln, ...), custom_call_target="tpu_custom_call" | custom-call | tf_op jit(solution)/shard_map/place/pallas_call | solution.py:806
